TPU v7x, 256 devices: a 8x8x2 block of a 8x8x16 slice. The times are simulated.
256 devices in a mesh: groups: 2 (over z), expert: 64 (over y, x), tensor: 2 (over core).
Axes of the slice: x: 8, y: 8, z: 2, core: 2. Of those that a mesh axis runs over, the one named last changes fastest.
The devices are a block of a 8x8x16 slice.
Arguments:
- hidden_in: bfloat16 [2048, 3584], P(('groups', 'expert')), parts along dimension 0, may hold values from -6 to 6
- batch_len: int32 [2], P('groups'), parts along dimension 0, may hold values from 256 to 1024
- expert_ids: int32 [2048, 8], P(('groups', 'expert')), parts along dimension 0, may hold values from 0 to 63, all different within a row; in each aligned block of 16 rows (0 to 15, 16 to 31, ...) at most 3 rows name the same one
- gate_num: int32 [2048, 8], P(('groups', 'expert')), parts along dimension 0, may hold values from 1 to 1024
- w_gate: bfloat16 [64, 3584, 1024], P('expert', None, 'tensor'), may hold values from -0.09375 to 0.09375
- w_up: bfloat16 [64, 3584, 1024], P('expert', None, 'tensor'), may hold values from -0.09375 to 0.09375
- w_down: bfloat16 [64, 1024, 3584], P('expert', 'tensor'), may hold values from -0.1875 to 0.1875
- q_latent: bfloat16 [4, 64, 512], P('groups', 'tensor'), parts along dimension 0, may hold values from -117 to 117
- q_rope: bfloat16 [4, 64, 64], P('groups', 'tensor'), parts along dimension 0, may hold values from -6 to 6
- kv_latent: bfloat16 [4, 8192, 512], P('groups', 'expert'), parts along dimension 0, may hold values from -4 to 4
- kv_rope: bfloat16 [4, 64, 8192], P('groups', None, 'expert'), parts along dimension 0, may hold values from -4 to 4
- ctx_len: int32 [4], P('groups'), parts along dimension 0, may hold values from 1 to 8192, as said below
Outputs:
- moe_out: bfloat16 [2048, 3584], P(('groups', 'expert')), parts along dimension 0
- attn_out: bfloat16 [4, 64, 512], P('groups', 'tensor'), parts along dimension 0
There are 2 independent parts, one for each index of `groups`. A program takes and returns all parts, laid end to end along the dimension named above; an argument that names none is the same for every part. Nothing has to cross between parts.
Inputs may be any that keep to these rules, and one draw needn't show every extreme that they name: `expert_ids`: each row names 8 different experts; the 16 rows of one index of the expert axis name any one expert at most 3 times. `batch_len`: the live slots are the first ones of the replica. `ctx_len`: the first request's context fills all 8192 positions.
All inputs are finite; a program needn't handle non-finite values.
Results may differ from a plain program's by a relative error of at most 0.0028.
The roundings to bfloat16 on the way count: a program that leaves them out, or rounds other values in their place, can miss the bound.
Values may be sent and summed in bfloat16 or wider, within the bound.
No kernel may reach another device: no remote copies, remote signals or barrier semaphores. Data moves between devices by JAX's collectives and lax.ppermute only.
A program may use at most 64 MiB of HBM per device.

v0:
```python
import jax
import jax.numpy as jnp
from jax import lax
from jax.sharding import Mesh
from jax.sharding import PartitionSpec as P

EXPERT = ("expert_0", "expert_1")
GROUPS_EXPERT = ("groups", "expert_0", "expert_1")


gate_denominator = 1024.0
softmax_scale = 192.0 ** (-0.5)


def joined_along(parts, dim):
    parts = jnp.moveaxis(parts, 0, dim)
    shape = parts.shape
    return parts.reshape(*shape[:dim], shape[dim] * shape[dim + 1], *shape[dim + 2 :])


def sent_to_all(value, axis):
    copies = jnp.broadcast_to(value, (lax.axis_size(axis), *value.shape))
    return lax.all_to_all(copies, axis, split_axis=0, concat_axis=0, tiled=True)


def gathered_copies(value, axis, dim):
    return joined_along(sent_to_all(value, axis), dim)


def exchange_in_groups(value, axis, split_dim, concat_dim, work, item_dim, out_dim):
    items = jax.tree.leaves(value)[0].shape[item_dim]
    count = 2 if items % 2 == 0 else 1
    finished = []
    for k in range(count):
        group = jax.tree.map(
            lambda a: lax.slice_in_dim(
                a, k * (items // count), (k + 1) * (items // count), axis=item_dim
            ),
            value,
        )
        finished.append(
            work(
                lax.all_to_all(
                    group, axis, split_axis=split_dim, concat_axis=concat_dim, tiled=True
                )
            )
        )
    return jax.tree.map(lambda *parts: jnp.concatenate(parts, axis=out_dim), *finished)


def in_blocks(value, dim, size):
    shape = value.shape
    parts = value.reshape(*shape[:dim], size, shape[dim] // size, *shape[dim + 1 :])
    return jnp.moveaxis(parts, dim, 0)


def summed_on_arrival(value, axis, dim):
    parts = in_blocks(value, dim, lax.axis_size(axis))
    arrived = lax.all_to_all(parts, axis, split_axis=0, concat_axis=0, tiled=True)
    return arrived.sum(axis=0)


def collected_together(value, axis):
    leaves = jax.tree.leaves(value)
    order = sorted(range(len(leaves)), key=lambda k: -leaves[k].size)
    width = (1, *leaves[order[0]].shape)[-1]
    lines = [
        jnp.pad(leaves[k].reshape(-1), (0, -leaves[k].size % width)).reshape(-1, width)
        for k in order
    ]
    both, at, found = (lax.all_gather(jnp.concatenate(lines), axis), 0, {})
    for k, line in zip(order, lines):
        slab = both[:, at : at + len(line)].reshape(len(both), -1)
        found[k] = slab[:, : leaves[k].size].reshape(-1, *leaves[k].shape)
        at += len(line)
    numbers = iter(range(len(leaves)))
    return jax.tree.map(lambda _: found[next(numbers)], value)


def combined_by_axis(value, axes, combine):
    for axis in axes:
        pieces = collected_together(value, axis)
        value = jax.tree.map(lambda part: part[0], pieces)
        for k in range(1, lax.axis_size(axis)):
            value = combine(value, jax.tree.map(lambda part: part[k], pieces))
    return value


def join_parts(first, second):
    peak = jnp.maximum(first[0], second[0])
    left = jnp.exp(first[0] - peak)
    right = jnp.exp(second[0] - peak)
    total = first[1] * left + second[1] * right
    weighted = first[2] * left[..., None] + second[2] * right[..., None]
    return (peak, total, weighted)


def local(
    hidden_in,
    batch_len,
    expert_ids,
    gate_num,
    w_gate,
    w_up,
    w_down,
    q_latent,
    q_rope,
    kv_latent,
    kv_rope,
    ctx_len,
):
    owners = lax.axis_size(EXPERT)
    tok_rows, width = hidden_in.shape
    topk = expert_ids.shape[1]
    capacity = min(tok_rows, max(2, 3 * tok_rows * topk // (2 * owners)))
    first_row = lax.axis_index(EXPERT) * tok_rows
    live = first_row + jnp.arange(tok_rows, dtype=jnp.int32) < batch_len[0]
    flat_expert = expert_ids.reshape(-1)
    live_pick = jnp.repeat(live, topk)
    onehot = (
        (flat_expert[:, None] == jnp.arange(owners, dtype=jnp.int32)[None, :]) & live_pick[:, None]
    ).astype(jnp.int32)
    ranking = jnp.cumsum(onehot, axis=0) - 1
    slot = jnp.sum(onehot * ranking, axis=1)
    target = jnp.where(live_pick, flat_expert * capacity + slot, owners * capacity)
    half_width = width // lax.axis_size("tensor")
    source = lax.dynamic_slice_in_dim(
        hidden_in, lax.axis_index("tensor") * half_width, half_width, 1
    )
    picked = jnp.repeat(source, topk, axis=0)
    packed = (
        jnp.zeros((owners * capacity, source.shape[1]), jnp.bfloat16)
        .at[target]
        .set(picked, mode="drop")
    )
    packed = packed.reshape(owners, capacity, source.shape[1])

    def expert_rows(rows):
        rows = gathered_copies(rows, "tensor", 2)
        count = rows.shape[1]
        flat = rows.reshape(-1, width)
        gate = jnp.dot(flat, w_gate[0], preferred_element_type=jnp.float32)
        upper = jnp.dot(flat, w_up[0], preferred_element_type=jnp.float32)
        hidden = (jax.nn.silu(gate) * upper).astype(jnp.bfloat16)
        return jnp.dot(hidden, w_down[0], preferred_element_type=jnp.float32).reshape(
            owners, count, width
        )

    partial_value = exchange_in_groups(packed, EXPERT, 0, 0, expert_rows, 1, 1)
    weight = jnp.where(live_pick, gate_num.reshape(-1).astype(jnp.float32) / gate_denominator, 0.0)
    back_index = jnp.where(live_pick, target, 0)
    share = summed_on_arrival(partial_value, "tensor", 2).astype(jnp.bfloat16)
    back = lax.all_to_all(share, EXPERT, split_axis=0, concat_axis=0, tiled=True)
    rows = back.reshape(owners * capacity, back.shape[2])[back_index].astype(jnp.float32)
    scaled = (rows * weight[:, None]).reshape(tok_rows, topk, back.shape[2])
    moe_out = gathered_copies(jnp.sum(scaled, axis=1).astype(jnp.bfloat16), "tensor", 1)
    ctx_dev = kv_latent.shape[1]
    position = lax.axis_index(EXPERT) * ctx_dev + jnp.arange(ctx_dev, dtype=jnp.int32)
    valid_pos = position[None, :] < ctx_len[:, None]
    scores = jnp.einsum("bhl,bpl->bhp", q_latent, kv_latent, preferred_element_type=jnp.float32)
    scores = scores + jnp.einsum(
        "bhr,brp->bhp", q_rope, kv_rope, preferred_element_type=jnp.float32
    )
    scores = jnp.where(valid_pos[:, None, :], scores * softmax_scale, -1e30)
    peak = jnp.max(scores, axis=2)
    probs = jnp.where(valid_pos[:, None, :], jnp.exp(scores - peak[..., None]), 0.0)
    total = jnp.sum(probs, axis=2)
    weighted = jnp.einsum(
        "bhp,bpl->bhl", probs.astype(jnp.bfloat16), kv_latent, preferred_element_type=jnp.float32
    )
    peak, total, weighted = combined_by_axis((peak, total, weighted), EXPERT, join_parts)
    attn_out = (weighted / total[..., None]).astype(jnp.bfloat16)
    return (moe_out, attn_out)


def solution(mesh):
    finer = Mesh(
        mesh.devices.reshape(mesh.shape["groups"], 8, 8, mesh.shape["tensor"]),
        ("groups", "expert_0", "expert_1", "tensor"),
    )
    in_specs = (
        P(GROUPS_EXPERT, None),
        P("groups"),
        P(GROUPS_EXPERT, None),
        P(GROUPS_EXPERT, None),
        P(EXPERT, None, "tensor"),
        P(EXPERT, None, "tensor"),
        P(EXPERT, "tensor", None),
        P("groups", "tensor", None),
        P("groups", "tensor", None),
        P("groups", EXPERT, None),
        P("groups", None, EXPERT),
        P("groups"),
    )
    out_specs = (P(GROUPS_EXPERT, None), P("groups", "tensor", None))
    return jax.shard_map(local, mesh=finer, in_specs=in_specs, out_specs=out_specs, check_vma=False)
```

profile of v0, /device:TPU:513, one launch (start us, length us, event | category | flops | bytes accessed | tf_op | source)
XLA Modules:
  0.0 166.3 jit_solution(2754419291117256892)
XLA Ops:
  7.3 0.9 copy-done
  8.1 1.0 fusion.91
  9.1 0.8 broadcast_compare_fusion
  9.9 1.0 fusion.90
  10.9 0.1 reshape.992
  11.0 0.2 fusion.41
  11.1 0.2 fusion.43
  11.3 0.1 reshape.994
  11.4 0.7 maximum_bitcast_fusion
  12.2 0.7 broadcast_multiply_fusion
  12.9 0.8 copy.53
  14.4 0.1 reshape.986
  14.5 0.1 and.13
  14.7 0.1 mul.454
  14.8 0.1 eq.15
  14.8 0.1 fusion.40
  15.0 0.2 reduce_window_sum.11
  15.1 0.2 select_reduce_fusion
  15.3 0.8 constant_dynamic-slice_fusion
  16.2 1.5 scatter_custom_fusion
  17.7 1.2 reshape.988
  18.8 21.8 %all-to-all-start = ((bf16[64,3,1792]{2,1,0:T(4,128)(2,1)}), bf16[64,3,1792]{2,1,0:T(4,128)(2,1)S(1)}, u32[]{:S(2)}, u32[]{:S(2)}) async-start(bf16[64,3,1792]{2,1,0:T(4,128)(2,1)} %reshape.988), calls=%async_computation | async-start | bytes 1835008 | tf_op jit(solution)/shard_map/all_to_all | solution.py:43
  40.7 5.9 %copy.67 = bf16[3584,512]{1,0:T(8,128)(2,1)} copy(bf16[3584,512]{0,1:T(8,128)(2,1)} %bitcast.322) | data formatting | bytes 7340032 | tf_op jit(solution)/shard_map/dot_general | solution.py:145
  46.6 13.1 %all-to-all-done = bf16[64,3,1792]{2,1,0:T(4,128)(2,1)S(1)} async-done(((bf16[64,3,1792]{2,1,0:T(4,128)(2,1)}), bf16[64,3,1792]{2,1,0:T(4,128)(2,1)S(1)}, u32[]{:S(2)}, u32[]{:S(2)}) %all-to-all-start) | async-done | bytes 688160 | tf_op jit(solution)/shard_map/all_to_all | solution.py:43
  59.8 0.1 broadcast_in_dim.41
  59.9 13.1 %all_to_all.25 = bf16[2,64,3,1792]{3,1,2,0:T(8,128)(2,1)S(1)} all-to-all(bf16[2,64,3,1792]{3,1,2,0:T(8,128)(2,1)S(1)} %broadcast_in_dim.41), channel_id=1, replica_groups=mesh['groups'=2,'expert_0'=8,'expert_1'=8,'tensor'=2] {'tensor'}, dimensions={0} | all-to-all | bytes 2752512 | tf_op jit(solution)/shard_map/all_to_all | solution.py:23
  73.0 1.4 copy.56
  74.4 0.1 copy.74
  74.5 0.5 copy-done.1
  75.0 0.9 fusion.2
  75.9 6.2 %all-gather.7.cloned.1.call-done = f32[8,66,512]{2,1,0:T(8,128)} async-done(((f32[1,66,512]{2,1,0:T(8,128)}), f32[8,66,512]{2,1,0:T(8,128)}) %all-gather.7.cloned.1.call-update) | async-done | bytes 1081360 | tf_op jit(solution)/shard_map/all_gather | solution.py:71
  82.1 1.0 fusion.89
  83.2 1.5 fusion.19
  84.7 0.7 maximum_bitcast_fusion.1
  85.4 2.9 %fusion.7 = bf16[192,512]{1,0:T(8,128)(2,1)S(1)} fusion(bf16[192,3584]{1,0:T(8,128)(2,1)S(1)} %bitcast.319, bf16[1,3584,512]{2,1,0:T(8,128)(2,1)} %param.17, f32[192,512]{1,0:T(8,128)S(1)} %fusion.2), kind=kOutput, calls=%fused_computation.8 | convolution fusion | flops 705232896 | bytes 5636096 | tf_op jit(solution)/shard_map/dot_general | solution.py:143
  88.3 0.1 dot_general.26
  88.5 3.4 %convolution_bitcast_fusion = f32[2,64,3,1792]{3,1,0,2:T(8,128)S(1)} fusion(bf16[2,1792,512,1]{2,1,0,3:T(8,128)(2,1)} %bitcast.317, bf16[64,3,512,1]{2,1,0,3:T(4,128)(2,1)S(1)} %bitcast.323), kind=kOutput, calls=%fused_computation.6 | convolution fusion | flops 704643072 | bytes 6619136 | tf_op jit(solution)/shard_map/dot_general | solution.py:145
  91.8 0.2 copy.59
  92.1 10.2 %all_to_all.26 = f32[2,64,3,1792]{3,1,2,0:T(8,128)S(1)} all-to-all(f32[2,64,3,1792]{3,1,2,0:T(8,128)S(1)} %copy.59), channel_id=1, replica_groups=mesh['groups'=2,'expert_0'=8,'expert_1'=8,'tensor'=2] {'tensor'}, dimensions={0} | all-to-all | bytes 5505024 | tf_op jit(solution)/shard_map/all_to_all | solution.py:59
  102.2 1.2 reduce_sum.40
  103.5 2.6 %copy.61 = bf16[64,3,1792]{2,1,0:T(4,128)(2,1)} copy(bf16[64,3,1792]{2,0,1:T(8,128)(2,1)} %reduce_sum.40) | data formatting | bytes 1376256 | tf_op jit(solution)/shard_map/convert_element_type | solution.py:152
  106.1 10.6 %all-to-all-start.3 = ((bf16[64,3,1792]{2,1,0:T(4,128)(2,1)}), bf16[64,3,1792]{2,1,0:T(4,128)(2,1)S(1)}, u32[]{:S(2)}, u32[]{:S(2)}) async-start(bf16[64,3,1792]{2,1,0:T(4,128)(2,1)} %copy.61), calls=%async_computation.3 | async-start | bytes 1835008 | tf_op jit(solution)/shard_map/all_to_all | solution.py:153
  116.7 30.1 %all-to-all-done.3 = bf16[64,3,1792]{2,1,0:T(4,128)(2,1)S(1)} async-done(((bf16[64,3,1792]{2,1,0:T(4,128)(2,1)}), bf16[64,3,1792]{2,1,0:T(4,128)(2,1)S(1)}, u32[]{:S(2)}, u32[]{:S(2)}) %all-to-all-start.3) | async-done | bytes 688160 | tf_op jit(solution)/shard_map/all_to_all | solution.py:153
  146.8 0.6 reshape.989
  147.4 0.9 gather_fusion
  148.4 0.4 fusion.12
  148.8 5.4 %all_to_all.27 = bf16[2,16,1792]{2,1,0:T(8,128)(2,1)S(1)} all-to-all(bf16[2,16,1792]{2,1,0:T(8,128)(2,1)S(1)} %broadcast_in_dim.43), channel_id=1, replica_groups=mesh['groups'=2,'expert_0'=8,'expert_1'=8,'tensor'=2] {'tensor'}, dimensions={0} | all-to-all | bytes 229376 | tf_op jit(solution)/shard_map/all_to_all | solution.py:23
  154.2 0.7 copy.73
  154.9 1.0 fusion.87
  155.9 0.1 squeeze.207
  156.0 0.1 squeeze.206
  156.1 0.1 squeeze.205
  156.2 0.1 squeeze.204
  156.2 0.1 squeeze.203
  156.3 0.1 squeeze.202
  156.4 0.1 squeeze.201
  156.6 0.1 squeeze.185
  156.7 0.1 squeeze.194
  156.8 0.1 squeeze.192
  156.9 0.1 squeeze.190
  156.9 0.1 squeeze.188
  157.0 0.1 squeeze.186
  157.3 1.4 fusion.88
  158.7 0.8 divide_convert_fusion
  (35 shorter events, 1.0 us)
Async XLA Ops:
  7.2 1.0 copy-start
  7.2 74.9 %all-gather.7.cloned.1.call-start = ((), (), s32[]{:S(2)}) async-start(), calls=%async_computation.5 | async-start | bytes 1327104 | tf_op jit(solution)/shard_map/all_gather | solution.py:71
  18.8 40.9 %all-to-all-start = ((bf16[64,3,1792]{2,1,0:T(4,128)(2,1)}), bf16[64,3,1792]{2,1,0:T(4,128)(2,1)S(1)}, u32[]{:S(2)}, u32[]{:S(2)}) async-start(bf16[64,3,1792]{2,1,0:T(4,128)(2,1)} %reshape.988), calls=%async_computation | async-start | bytes 1835008 | tf_op jit(solution)/shard_map/all_to_all | solution.py:43
  40.6 114.3 %all-gather.9.cloned.1.call-start = ((), (), s32[]{:S(2)}) async-start(), calls=%async_computation.6 | async-start | bytes 1327104 | tf_op jit(solution)/shard_map/all_gather | solution.py:71
  73.0 2.1 %copy-start.1 = (bf16[1,3584,512]{2,1,0:T(8,128)(2,1)S(1)}, bf16[1,3584,512]{2,1,0:T(8,128)(2,1)}, u32[]{:S(2)}) copy-start(bf16[1,3584,512]{2,1,0:T(8,128)(2,1)} %param.16) | copy-start | bytes 11010052
  102.2 14.4 %copy-start.2 = (s32[16,8]{0,1:T(8,128)S(1)}, s32[16,8]{0,1:T(8,128)}, u32[]{:S(2)}) copy-start(s32[16,8]{0,1:T(8,128)} %param.15) | copy-start | bytes 1540
  106.1 40.8 %all-to-all-start.3 = ((bf16[64,3,1792]{2,1,0:T(4,128)(2,1)}), bf16[64,3,1792]{2,1,0:T(4,128)(2,1)S(1)}, u32[]{:S(2)}, u32[]{:S(2)}) async-start(bf16[64,3,1792]{2,1,0:T(4,128)(2,1)} %copy.61), calls=%async_computation.3 | async-start | bytes 1835008 | tf_op jit(solution)/shard_map/all_to_all | solution.py:153
Sparse Core Ops, SparseCore 0:
  12.3 69.7 all-gather.6
  85.5 49.3 all-gather.8
where the time goes:
time: 167 us; the launch traced here: 166 us
  waiting for transfers between devices  49.5 us (30%)
  starting transfers between devices  32.5 us (19%)
  blocking collectives  28.6 us (17%)
  local copies, waits for them, and re-layouts  23.9 us (14%)
  between operations  15 us (9%)
  matrix products  9.37 us (6%)
  other arithmetic  7.51 us (4%)
    all_to_all x1, waiting for transfers between devices, local(): lax.all_to_all(share, EXPERT, split_axis=0, concat_axis=0, tiled=True)  30.1 us
    all_to_all x1, starting transfers between devices, exchange_in_groups(): lax.all_to_all(group, axis, split_axis=split_dim, concat_axis=concat_dim,...  21.8 us
    all_to_all x2, blocking collectives, sent_to_all(): return lax.all_to_all(copies, axis, split_axis=0, concat_axis=0, tiled=True)  18.5 us
    all_to_all x1, waiting for transfers between devices, exchange_in_groups(): lax.all_to_all(group, axis, split_axis=split_dim, concat_axis=concat_dim,...  13.1 us
    all_to_all x1, starting transfers between devices, local(): lax.all_to_all(share, EXPERT, split_axis=0, concat_axis=0, tiled=True)  10.6 us
    all_to_all x1, blocking collectives, summed_on_arrival(): lax.all_to_all(parts, axis, split_axis=0, concat_axis=0, tiled=True)  10.2 us
    all_gather x2, waiting for transfers between devices, collected_together(): both, at, found = (lax.all_gather(jnp.concatenate(lines), axis), 0, {})  6.21 us
    dot_general x2, local copies, waits for them, and re-layouts, expert_rows(): jnp.dot(hidden, w_down[0], preferred_element_type=jnp.float32)  6.04 us
  transfers between devices with their start and end apart: 4, of which 3 were waited for; matrix products, arithmetic and copies ran while one was open for 17% of the time, Pallas kernels for 0%

commit v1 on v0

v1 whole, which is shorter than its diff:
```python
import functools

import jax
import jax.numpy as jnp
from jax import lax
from jax.experimental import pallas as pl
from jax.experimental.pallas import tpu as pltpu
from jax.sharding import PartitionSpec as P

SUB = 8
CAP = 3
bf16 = jnp.bfloat16
f32 = jnp.float32
softmax_scale = 192.0 ** (-0.5)
gate_denominator = 1024.0
INTERPRET = False


def iota(shape, dim):
    return lax.broadcasted_iota(jnp.int32, shape, dim)


def dot(a, b):
    return jnp.dot(a, b, preferred_element_type=f32)


def dot_nt(a, b):
    return lax.dot_general(a, b, (((1,), (1,)), ((), ())), preferred_element_type=f32)


def ones_where(condition, dtype=bf16):
    return jnp.where(condition, 1.0, 0.0).astype(dtype)


def in_three(value):
    high = value.astype(bf16).astype(f32)
    middle = (value - high).astype(bf16).astype(f32)
    return high, middle, (value - high - middle).astype(bf16).astype(f32)


def routing(ids, owners, first_row, live_count):
    rows, topk = ids.shape
    lane = iota((rows, owners), 1)
    picks = [ids[:, k : k + 1] == lane for k in range(topk)]
    live = first_row + iota((rows, owners), 0) < live_count
    match = sum(ones_where(p, f32) for p in picks)
    match = jnp.where(live, match, 0.0)
    before = ones_where(iota((rows, rows), 1) < iota((rows, rows), 0))
    return picks, match, dot(before, match.astype(bf16))


def pack_kernel(where_ref, len_ref, ctx_ref, hid_ref, ids_ref, ql_ref, qr_ref, kl_ref, kr_ref, out_ref):
    expert, tensor = where_ref[0], where_ref[1]
    total_rows, width = out_ref.shape
    owners = total_rows // SUB
    piece = width // CAP
    tok = hid_ref.shape[0]
    half = hid_ref.shape[1] // 2
    batch, heads, lat = ql_ref.shape
    ctx_dev = kl_ref.shape[1]

    parts = []
    for b in range(batch):
        latent = kl_ref[b]
        s = dot_nt(ql_ref[b], latent) + dot(qr_ref[b], kr_ref[b])
        valid = expert * ctx_dev + iota((heads, ctx_dev), 1) < ctx_ref[b]
        s = jnp.where(valid, s * softmax_scale, -1e30)
        top = jnp.max(s, axis=1, keepdims=True)
        p = jnp.where(valid, jnp.exp(s - top), 0.0)
        total = jnp.sum(p, axis=1, keepdims=True)
        mean = dot(p.astype(bf16), latent) / jnp.where(total > 0.0, total, 1.0)
        at = iota((heads, width - lat), 1)
        stats = jnp.zeros((heads, width - lat), f32)
        for k, number in enumerate(in_three(top) + in_three(total)):
            stats = jnp.where(at == k, number, stats)
        parts.append(jnp.concatenate([mean, stats], axis=1).astype(bf16))
    attn = jnp.concatenate(parts, axis=0)

    hidden = hid_ref[...]
    source = jnp.where(tensor == 0, hidden[:, :half], hidden[:, half:])
    stacked = [source[:, k * piece : (k + 1) * piece] for k in range(half // piece)]
    stacked.append(jnp.zeros((tok, piece), bf16))
    stacked = jnp.concatenate(stacked, axis=0)
    _, match, rank = routing(ids_ref[...], owners, expert * tok, len_ref[0])
    mine = [jnp.where(rank == c, match, 0.0).astype(bf16) for c in range(CAP)]
    tiled = jnp.concatenate([m for m in mine for _ in range(SUB)], axis=0)
    spread = ones_where(iota((total_rows, owners), 0) // SUB == iota((total_rows, owners), 1))
    chosen = dot_nt(spread, tiled)
    block = SUB * tok
    row, col = iota((total_rows, block), 0), iota((total_rows, block), 1)
    kept = (row % SUB == col // tok) & (col < block - tok)
    last = ones_where(
        iota((total_rows, owners), 0) == iota((total_rows, owners), 1) * SUB + (SUB - 1)
    )
    for c in range(CAP):
        lhs = jnp.where(kept, chosen[:, c * block : (c + 1) * block], 0.0).astype(bf16)
        at = slice(c * piece, (c + 1) * piece)
        out_ref[:, at] = (dot(lhs, stacked) + dot(last, attn[:, at])).astype(bf16)


def ffn_kernel(
    where_ref, own_ref, other_ref, wg_ref, wu_ref, wd_ref,
    keep_ref, send_ref, attn_ref,
    wg, wu, wd, rows, sems,
):
    tensor = where_ref[1]
    total_rows, width = own_ref.shape
    owners = total_rows // SUB
    piece = width // CAP
    half = wg_ref.shape[1] // 2
    lat = attn_ref.shape[1]
    first = [pl.multiple_of(tensor * half, half), pl.multiple_of((1 - tensor) * half, half)]

    copies = []
    for h in range(2):
        copies.append(pltpu.make_async_copy(wg_ref.at[0, pl.ds(first[h], half), :], wg.at[h], sems.at[2 * h]))
        copies.append(pltpu.make_async_copy(wu_ref.at[0, pl.ds(first[h], half), :], wu.at[h], sems.at[2 * h + 1]))
    for h in range(2):
        copies.append(pltpu.make_async_copy(wd_ref.at[0, :, pl.ds(first[1 - h], half)], wd.at[1 - h], sems.at[4 + h]))
    for copy in copies:
        copy.start()

    row, col = iota((total_rows, total_rows), 0), iota((total_rows, total_rows), 1)
    order = ones_where(col == (row % owners) * SUB + row // owners)
    for h, ref in enumerate((own_ref, other_ref)):
        sorted_rows = dot(order, ref[...])
        for k in range(SUB - 1):
            for c in range(CAP):
                rows[h, c * owners : (c + 1) * owners, k * piece : (k + 1) * piece] = sorted_rows[
                    k * owners : (k + 1) * owners, c * piece : (c + 1) * piece
                ].astype(bf16)
        if h == 0:
            arrived = sorted_rows[(SUB - 1) * owners :]
            stats = [arrived[:, lat + k : lat + k + 1] for k in range(6)]
            top = stats[0] + stats[1] + stats[2]
            total = stats[3] + stats[4] + stats[5]
            share = jnp.exp(top - jnp.max(top, axis=0, keepdims=True)) * total
            weighted = jnp.sum(share * arrived[:, :lat], axis=0, keepdims=True)
            done = weighted / jnp.sum(share, axis=0, keepdims=True)
            attn_ref[...] = jnp.broadcast_to(done, attn_ref.shape).astype(bf16)

    copies[0].wait()
    gate = dot(rows[0], wg[0])
    copies[1].wait()
    upper = dot(rows[0], wu[0])
    copies[2].wait()
    gate = gate + dot(rows[1], wg[1])
    copies[3].wait()
    upper = upper + dot(rows[1], wu[1])
    hidden = (gate / (1.0 + jnp.exp(-gate)) * upper).astype(bf16)
    copies[4].wait()
    send_ref[...] = dot(hidden, wd[1])
    copies[5].wait()
    keep_ref[...] = dot(hidden, wd[0])


def back_kernel(keep_ref, come_ref, attn_ref, out_ref, value):
    total_rows, width = out_ref.shape
    owners = total_rows // SUB
    piece = width // CAP
    lat = attn_ref.shape[1]
    for k in range(SUB - 1):
        for c in range(CAP):
            at = (slice(c * owners, (c + 1) * owners), slice(k * piece, (k + 1) * piece))
            value[k * owners : (k + 1) * owners, c * piece : (c + 1) * piece] = (
                keep_ref[at] + come_ref[at]
            ).astype(bf16)
    value[(SUB - 1) * owners :, :lat] = jnp.broadcast_to(attn_ref[0:1, :], (owners, lat))
    value[(SUB - 1) * owners :, lat:] = jnp.zeros((owners, width - lat), bf16)
    row, col = iota((total_rows, total_rows), 0), iota((total_rows, total_rows), 1)
    order = ones_where(col == (row % SUB) * owners + row // SUB)
    out_ref[...] = dot(order, value[...]).astype(bf16)


def sum_kernel(where_ref, len_ref, back_ref, ids_ref, gate_ref, moe_ref, attn_ref):
    expert = where_ref[0]
    total_rows, width = back_ref.shape
    owners = total_rows // SUB
    piece = width // CAP
    tok = ids_ref.shape[0]
    picks, match, rank = routing(ids_ref[...], owners, expert * tok, len_ref[0])
    gates = gate_ref[...]
    lower = gates % 8
    split = []
    for number in (gates - lower, lower):
        number = number.astype(f32)
        split.append(sum(jnp.where(p, number[:, k : k + 1], 0.0) for k, p in enumerate(picks)))
    spread = ones_where(iota((total_rows, owners), 0) // SUB == iota((total_rows, owners), 1))
    tiled = []
    for c in range(CAP):
        for number in split:
            mine = jnp.where((rank == c) & (match > 0.0), number, 0.0).astype(bf16)
            tiled.extend([mine] * SUB)
    chosen = dot_nt(jnp.concatenate(tiled, axis=0), spread)
    block = SUB * tok
    row, col = iota((2 * block, total_rows), 0), iota((2 * block, total_rows), 1)
    kept = row % block // tok == col % SUB
    summed = jnp.zeros((2 * block, piece), f32)
    for c in range(CAP):
        lhs = jnp.where(kept, chosen[c * 2 * block : (c + 1) * 2 * block], 0.0).astype(bf16)
        summed = summed + dot(lhs, back_ref[:, c * piece : (c + 1) * piece])
    summed = (summed[:block] + summed[block:]) * (1.0 / gate_denominator)
    for k in range(SUB - 1):
        moe_ref[:, k * piece : (k + 1) * piece] = summed[k * tok : (k + 1) * tok].astype(bf16)
    lat = attn_ref.shape[1]
    last = ones_where(
        iota((owners, total_rows), 1) == iota((owners, total_rows), 0) * SUB + (SUB - 1)
    )
    attn_ref[...] = dot(last, back_ref[:, :lat]).astype(bf16)


def vmem():
    return pl.BlockSpec(memory_space=pltpu.VMEM)


def smem():
    return pl.BlockSpec(memory_space=pltpu.SMEM)


def hbm():
    return pl.BlockSpec(memory_space=pl.ANY)


def call(kernel, out_shape, in_specs, scratch=(), vmem_mib=32):
    several = isinstance(out_shape, (tuple, list))
    return pl.pallas_call(
        kernel,
        out_shape=out_shape,
        in_specs=in_specs,
        out_specs=tuple(vmem() for _ in out_shape) if several else vmem(),
        scratch_shapes=list(scratch),
        compiler_params=pltpu.CompilerParams(vmem_limit_bytes=vmem_mib << 20),
        interpret=INTERPRET,
    )


def local(
    hidden_in,
    batch_len,
    expert_ids,
    gate_num,
    w_gate,
    w_up,
    w_down,
    q_latent,
    q_rope,
    kv_latent,
    kv_rope,
    ctx_len,
):
    owners = lax.axis_size("expert")
    tok, features = hidden_in.shape
    half = features // 2
    hidden_units = w_gate.shape[2]
    batch, heads, lat = q_latent.shape
    total_rows = owners * SUB
    width = CAP * half // (SUB - 1)
    tensor = lax.axis_index("tensor")
    where = jnp.stack([lax.axis_index("expert"), tensor]).astype(jnp.int32)
    swap = [(0, 1), (1, 0)]

    def exchanged(packed):
        whole = packed.reshape(owners, SUB, width)
        return lax.all_to_all(whole, "expert", 0, 0, tiled=True).reshape(total_rows, width)

    packed = call(
        pack_kernel,
        jax.ShapeDtypeStruct((total_rows, width), bf16),
        [smem(), smem(), smem(), vmem(), vmem(), vmem(), vmem(), vmem(), vmem()],
    )(where, batch_len, ctx_len, hidden_in, expert_ids, q_latent, q_rope, kv_latent, kv_rope)
    own = exchanged(packed)
    other = lax.ppermute(own, "tensor", swap)
    slots = CAP * owners
    keep, send, attn = call(
        ffn_kernel,
        (
            jax.ShapeDtypeStruct((slots, half), f32),
            jax.ShapeDtypeStruct((slots, half), f32),
            jax.ShapeDtypeStruct((16, lat), bf16),
        ),
        [smem(), vmem(), vmem(), hbm(), hbm(), hbm()],
        [
            pltpu.VMEM((2, half, hidden_units), bf16),
            pltpu.VMEM((2, half, hidden_units), bf16),
            pltpu.VMEM((2, hidden_units, half), bf16),
            pltpu.VMEM((2, slots, half), bf16),
            pltpu.SemaphoreType.DMA((6,)),
        ],
        48,
    )(where, own, other, w_gate, w_up, w_down)
    come = lax.ppermute(send, "tensor", swap)
    returned = call(
        back_kernel,
        jax.ShapeDtypeStruct((total_rows, width), bf16),
        [vmem(), vmem(), vmem()],
        [pltpu.VMEM((total_rows, width), bf16)],
    )(keep, come, attn)
    back = exchanged(returned)
    moe_half, attn_out = call(
        sum_kernel,
        (
            jax.ShapeDtypeStruct((tok, half), bf16),
            jax.ShapeDtypeStruct((batch * heads, lat), bf16),
        ),
        [smem(), smem(), vmem(), vmem(), vmem()],
    )(where, batch_len, back, expert_ids, gate_num)
    moe_other = lax.ppermute(moe_half, "tensor", swap)
    moe_out = jnp.where(
        tensor == 0,
        jnp.concatenate([moe_half, moe_other], axis=1),
        jnp.concatenate([moe_other, moe_half], axis=1),
    )
    return moe_out, attn_out.reshape(batch, heads, lat)


def solution(mesh):
    both = ("groups", "expert")
    in_specs = (
        P(both, None),
        P("groups"),
        P(both, None),
        P(both, None),
        P("expert", None, "tensor"),
        P("expert", None, "tensor"),
        P("expert", "tensor", None),
        P("groups", "tensor", None),
        P("groups", "tensor", None),
        P("groups", "expert", None),
        P("groups", None, "expert"),
        P("groups"),
    )
    out_specs = (P(both, None), P("groups", "tensor", None))
    return jax.shard_map(local, mesh=mesh, in_specs=in_specs, out_specs=out_specs, check_vma=False)
```

time: 167 us -> 102 us (0.61)
  waiting for transfers between devices: 49.5 us -> 26.5 us
  local copies, waits for them, and re-layouts: 23.9 us -> 5.65 us
  starting transfers between devices: 32.5 us -> 17.1 us
  between operations: 15 us -> 1.34 us
  Pallas kernels: 0 us -> 11.8 us
  blocking collectives: 28.6 us -> 38.9 us
  matrix products: 9.37 us -> 0 us
  other arithmetic: 7.51 us -> 0.75 us
    all_to_all x2 -> x1, starting transfers between devices: 32.3 us -> 7.11 us  [exchanged(): lax.all_to_all(whole, 'expert', 0, 0, tiled=True).reshape(total_rows, width)]
    all_to_all x2 -> x1, waiting for transfers between devices: 43.2 us -> 20.9 us  [exchanged(): lax.all_to_all(whole, 'expert', 0, 0, tiled=True).reshape(total_rows, width)]
    pallas_call x0 -> x4, Pallas kernels: none -> 11.8 us  [the longest x1 6.33 us: local(): call(ffn_kernel, (jax.ShapeDtypeStruct((slots, half), f32), jax.ShapeDtyp...]
    all_to_all x3 -> x1, blocking collectives: 28.6 us -> 38.9 us  [exchanged(): lax.all_to_all(whole, 'expert', 0, 0, tiled=True).reshape(total_rows, width)]
    ppermute x0 -> x3, starting transfers between devices: none -> 10 us  [the longest x1 7.09 us: local(): other = lax.ppermute(own, 'tensor', swap)]
    dot_general x6 -> x0, matrix products: 9.37 us -> none  [the longest x1 3.38 us: expert_rows(): jnp.dot(hidden, w_down[0], preferred_element_type=jnp.float32)]
    all_gather x2 -> x0, waiting for transfers between devices: 6.21 us -> none  [collected_together(): both, at, found = (lax.all_gather(jnp.concatenate(lines), axis), 0, {})]
    dot_general x2 -> x0, local copies, waits for them, and re-layouts: 6.04 us -> none  [expert_rows(): jnp.dot(hidden, w_down[0], preferred_element_type=jnp.float32)]
  transfers between devices with their start and end apart: 4 -> 4, of which waited for: 3 -> 4; matrix products, arithmetic and copies ran while one was open for 17% -> 0% of each run, Pallas kernels for 0% -> 0%
where the time goes in v1:
time: 102 us
  blocking collectives  38.9 us (38%)
  waiting for transfers between devices  26.5 us (26%)
  starting transfers between devices  17.1 us (17%)
  Pallas kernels  11.8 us (12%)
  local copies, waits for them, and re-layouts  5.65 us (6%)
  between operations  1.34 us (1%)
    all_to_all x1, blocking collectives, exchanged(): lax.all_to_all(whole, 'expert', 0, 0, tiled=True).reshape(total_rows, width)  38.9 us
    all_to_all x1, waiting for transfers between devices, exchanged(): lax.all_to_all(whole, 'expert', 0, 0, tiled=True).reshape(total_rows, width)  20.9 us
    all_to_all x1, starting transfers between devices, exchanged(): lax.all_to_all(whole, 'expert', 0, 0, tiled=True).reshape(total_rows, width)  7.11 us
    ppermute x1, starting transfers between devices, local(): other = lax.ppermute(own, 'tensor', swap)  7.09 us
    pallas_call x1, Pallas kernels, local(): call(ffn_kernel, (jax.ShapeDtypeStruct((slots, half), f32), jax.ShapeDtyp...  6.33 us
    unnamed x16, local copies, waits for them, and re-layouts  5.65 us
    ppermute x1, waiting for transfers between devices, local(): come = lax.ppermute(send, 'tensor', swap)  2.76 us
    ppermute x1, starting transfers between devices, local(): moe_other = lax.ppermute(moe_half, 'tensor', swap)  2.43 us
  transfers between devices with their start and end apart: 4, of which 4 were waited for; matrix products, arithmetic and copies ran while one was open for 0% of the time, Pallas kernels for 0%

profile of v1, /device:TPU:513, one launch (start us, length us, event | category | flops | bytes accessed | tf_op | source)
XLA Modules:
  0.0 102.0 jit_solution(2140903976519021590)
XLA Ops:
  0.6 0.8 copy.14.ids_ref
  2.0 0.1 pad_add_fusion.where_ref
  2.1 0.0 copy-start
  2.1 0.9 copy-done
  3.1 0.0 copy-start.1
  3.1 0.9 copy-done.1
  4.0 0.0 copy-start.2
  4.0 0.8 copy-done.2
  4.8 0.0 copy-start.3
  4.8 0.8 copy-done.3
  5.6 0.0 copy-start.4
  5.6 0.7 copy-done.4
  6.3 0.0 copy-start.5
  6.3 0.7 copy-done.5
  6.9 1.8 %shard_map.131 = bf16[512,768]{1,0:T(8,128)(2,1)S(1)} custom-call(s32[2]{0:T(128)S(1)} %pad_add_fusion.where_ref, s32[1]{0:T(128)S(6)} %copy.17.len_ref, s32[2]{0:T(128)S(1)} %copy-done.5, bf16[16,3584]{1,0:T(8,128)(2,1)S(1)} %copy-done.1, s32[16,8]{1,0:T(8,128)S(1)} %copy.14.ids_ref, bf16[2,32,512]{2,1,0:T(8,128)(2,1)S(1)} %copy-done.2, ...), custom_call_target="tpu_custom_call" | custom-call | tf_op jit(solution)/shard_map/pallas_call | solution.py:266
  8.8 38.9 %all_to_all.10 = bf16[64,8,768]{2,1,0:T(8,128)(2,1)S(1)} all-to-all(bf16[64,8,768]{2,1,0:T(8,128)(2,1)S(1)} %bitcast.10), channel_id=1, replica_groups=mesh['groups'=2,'expert'=64,'tensor'=2] {'expert'}, dimensions={0} | all-to-all | bytes 1572864 | tf_op jit(solution)/shard_map/all_to_all | solution.py:264
  47.7 7.1 %collective-permute-start = (bf16[512,768]{1,0:T(8,128)(2,1)S(1)}, bf16[512,768]{1,0:T(8,128)(2,1)S(1)}, u32[]{:S(2)}, u32[]{:S(2)}) collective-permute-start(bf16[512,768]{1,0:T(8,128)(2,1)S(1)} %bitcast.7), channel_id=1, source_target_pairs={{0,1},{1,0},{2,3},{3,2},{4,5},{5,4},{6,7},{7,6},{8,9},{9,8},{10,11... | collective-permute-start | bytes 2359304 | tf_op jit(solution)/shard_map/ppermute | solution.py:272
  54.8 1.9 %collective-permute-done.other_ref = bf16[512,768]{1,0:T(8,128)(2,1)S(1)} collective-permute-done((bf16[512,768]{1,0:T(8,128)(2,1)S(1)}, bf16[512,768]{1,0:T(8,128)(2,1)S(1)}, u32[]{:S(2)}, u32[]{:S(2)}) %collective-permute-start) | collective-permute-done | bytes 786464 | tf_op jit(solution)/shard_map/ppermute | solution.py:272
  56.7 6.3 %shard_map.132 = (f32[192,1792]{1,0:T(8,128)S(1)}, f32[192,1792]{1,0:T(8,128)S(1)}, bf16[16,512]{1,0:T(8,128)(2,1)S(1)}) custom-call(s32[2]{0:T(128)S(1)} %pad_add_fusion.where_ref, bf16[512,768]{1,0:T(8,128)(2,1)S(1)} %bitcast.8, bf16[512,768]{1,0:T(8,128)(2,1)S(1)} %collective-permute-done.other_ref, bf16[1,3584,512]{2,1,0:T(8,128)(2,1)} %wg_ref.1, ...), custom_call_target="tpu_custom_call" | custom-call | tf_op jit(solution)/shard_map/pallas_call | solution.py:274
  63.0 0.0 copy-start.6
  63.0 0.5 collective-permute-start.1
  63.5 2.8 %collective-permute-done.1.come_ref = f32[192,1792]{1,0:T(8,128)S(1)} collective-permute-done((f32[192,1792]{1,0:T(8,128)S(1)}, f32[192,1792]{1,0:T(8,128)S(1)}, u32[]{:S(2)}, u32[]{:S(2)}) %collective-permute-start.1) | collective-permute-done | bytes 1376288 | tf_op jit(solution)/shard_map/ppermute | solution.py:291
  66.3 1.5 %shard_map.133 = bf16[512,768]{1,0:T(8,128)(2,1)} custom-call(f32[192,1792]{1,0:T(8,128)S(1)} %get-tuple-element.7.keep_ref, f32[192,1792]{1,0:T(8,128)S(1)} %collective-permute-done.1.come_ref, bf16[16,512]{1,0:T(8,128)(2,1)S(1)} %get-tuple-element.9.attn_ref), custom_call_target="tpu_custom_call" | custom-call | tf_op jit(solution)/shard_map/pallas_call | solution.py:292
  67.8 7.1 %all-to-all-start.1 = ((bf16[64,8,768]{2,1,0:T(8,128)(2,1)}), bf16[64,8,768]{2,1,0:T(8,128)(2,1)S(1)}, u32[]{:S(2)}, u32[]{:S(2)}) async-start(bf16[64,8,768]{2,1,0:T(8,128)(2,1)} %bitcast.4), calls=%async_computation.1 | async-start | bytes 1572864 | tf_op jit(solution)/shard_map/all_to_all | solution.py:264
  74.9 0.0 copy-done.6
  74.9 0.1 copy.16.gate_ref
  75.0 20.9 %all-to-all-done.1 = bf16[64,8,768]{2,1,0:T(8,128)(2,1)S(1)} async-done(((bf16[64,8,768]{2,1,0:T(8,128)(2,1)}), bf16[64,8,768]{2,1,0:T(8,128)(2,1)S(1)}, u32[]{:S(2)}, u32[]{:S(2)}) %all-to-all-start.1) | async-done | bytes 786464 | tf_op jit(solution)/shard_map/all_to_all | solution.py:264
  95.9 2.1 %shard_map.134 = (bf16[16,1792]{1,0:T(8,128)(2,1)S(1)}, bf16[64,512]{1,0:T(8,128)(2,1)}) custom-call(s32[2]{0:T(128)S(1)} %pad_add_fusion.where_ref, s32[1]{0:T(128)S(6)} %copy.17.len_ref, bf16[512,768]{1,0:T(8,128)(2,1)S(1)} %bitcast.9, s32[16,8]{1,0:T(8,128)S(1)} %copy.14.ids_ref, s32[16,8]{1,0:T(8,128)S(1)} %copy.16.gate_ref), custom_call_target="tpu_custom_call" | custom-call | tf_op jit(solution)/shard_map/pallas_call | solution.py:299
  98.0 2.4 %collective-permute-start.2 = (bf16[16,1792]{1,0:T(8,128)(2,1)S(1)}, bf16[16,1792]{1,0:T(8,128)(2,1)S(1)}, u32[]{:S(2)}, u32[]{:S(2)}) collective-permute-start(bf16[16,1792]{1,0:T(8,128)(2,1)S(1)} %get-tuple-element.10), channel_id=1, source_target_pairs={{0,1},{1,0},{2,3},{3,2},{4,5},{5,4},{6,7},{7,6},{8,9},{9,8},{10,11... | collective-permute-start | bytes 172040 | tf_op jit(solution)/shard_map/ppermute | solution.py:307
  100.4 0.9 collective-permute-done.2
  101.3 0.7 maximum_select_fusion
Async XLA Ops:
  2.1 1.0 copy-start
  3.1 0.9 copy-start.1
  4.0 0.8 copy-start.2
  4.8 0.8 copy-start.3
  5.6 0.7 copy-start.4
  6.3 0.7 copy-start.5
  47.7 9.0 %collective-permute-start = (bf16[512,768]{1,0:T(8,128)(2,1)S(1)}, bf16[512,768]{1,0:T(8,128)(2,1)S(1)}, u32[]{:S(2)}, u32[]{:S(2)}) collective-permute-start(bf16[512,768]{1,0:T(8,128)(2,1)S(1)} %bitcast.7), channel_id=1, source_target_pairs={{0,1},{1,0},{2,3},{3,2},{4,5},{5,4},{6,7},{7,6},{8,9},{9,8},{10,11... | collective-permute-start | bytes 2359304 | tf_op jit(solution)/shard_map/ppermute | solution.py:272
  63.0 11.9 %copy-start.6 = (s32[16,8]{0,1:T(8,128)S(1)}, s32[16,8]{0,1:T(8,128)}, u32[]{:S(2)}) copy-start(s32[16,8]{0,1:T(8,128)} %param.15) | copy-start | bytes 1540
  63.0 3.3 %collective-permute-start.1 = (f32[192,1792]{1,0:T(8,128)S(1)}, f32[192,1792]{1,0:T(8,128)S(1)}, u32[]{:S(2)}, u32[]{:S(2)}) collective-permute-start(f32[192,1792]{1,0:T(8,128)S(1)} %get-tuple-element.8), channel_id=1, source_target_pairs={{0,1},{1,0},{2,3},{3,2},{4,5},{5,4},{6,7},{7,6},{8,9},{9,8},{10,11... | collective-permute-start | bytes 4128776 | tf_op jit(solution)/shard_map/ppermute | solution.py:291
  67.8 28.1 %all-to-all-start.1 = ((bf16[64,8,768]{2,1,0:T(8,128)(2,1)}), bf16[64,8,768]{2,1,0:T(8,128)(2,1)S(1)}, u32[]{:S(2)}, u32[]{:S(2)}) async-start(bf16[64,8,768]{2,1,0:T(8,128)(2,1)} %bitcast.4), calls=%async_computation.1 | async-start | bytes 1572864 | tf_op jit(solution)/shard_map/all_to_all | solution.py:264
  98.0 3.3 %collective-permute-start.2 = (bf16[16,1792]{1,0:T(8,128)(2,1)S(1)}, bf16[16,1792]{1,0:T(8,128)(2,1)S(1)}, u32[]{:S(2)}, u32[]{:S(2)}) collective-permute-start(bf16[16,1792]{1,0:T(8,128)(2,1)S(1)} %get-tuple-element.10), channel_id=1, source_target_pairs={{0,1},{1,0},{2,3},{3,2},{4,5},{5,4},{6,7},{7,6},{8,9},{9,8},{10,11... | collective-permute-start | bytes 172040 | tf_op jit(solution)/shard_map/ppermute | solution.py:307

commit v2 on v1

v2 whole, which is shorter than its diff:
```python
import functools

import jax
import jax.numpy as jnp
from jax import lax
from jax.experimental import pallas as pl
from jax.experimental.pallas import tpu as pltpu
from jax.sharding import PartitionSpec as P

SUB = 8
CAP = 3
bf16 = jnp.bfloat16
f32 = jnp.float32
softmax_scale = 192.0 ** (-0.5)
gate_denominator = 1024.0
INTERPRET = False


def iota(shape, dim):
    return lax.broadcasted_iota(jnp.int32, shape, dim)


def dot(a, b):
    return jnp.dot(a, b, preferred_element_type=f32)


def dot_nt(a, b):
    return lax.dot_general(a, b, (((1,), (1,)), ((), ())), preferred_element_type=f32)


def ones_where(condition, dtype=bf16):
    return jnp.where(condition, 1.0, 0.0).astype(dtype)


def in_three(value):
    high = value.astype(bf16).astype(f32)
    middle = (value - high).astype(bf16).astype(f32)
    return high, middle, (value - high - middle).astype(bf16).astype(f32)


def routing(ids_t, owners, tok, live_count):
    topk = ids_t.shape[0]
    lanes = SUB * tok
    repeat = ones_where(iota((tok, lanes), 1) % tok == iota((tok, lanes), 0))
    ids = dot(ids_t.astype(f32).astype(bf16), repeat)
    row = iota((owners, lanes), 0).astype(f32)
    picks = [ids[k : k + 1, :] == row for k in range(topk)]
    live = lax.axis_index("expert") * tok + iota((owners, lanes), 1) % tok < live_count
    match = sum(ones_where(p, f32) for p in picks)
    match = jnp.where(live, match, 0.0)
    first, second = iota((lanes, lanes), 0), iota((lanes, lanes), 1)
    before = ones_where((first // tok == second // tok) & (first < second))
    return repeat, picks, match, dot(match.astype(bf16), before)


def pack_kernel(
    len_ref, ctx_ref, hid_hbm, ids_hbm, ql_hbm, qr_hbm, kl_hbm, kr_hbm,
    out_ref,
    hid_ref, ids_ref, ql_ref, qr_ref, kl_ref, kr_ref, sems,
):
    pairs = (
        (ql_hbm, ql_ref), (kl_hbm, kl_ref), (qr_hbm, qr_ref),
        (kr_hbm, kr_ref), (ids_hbm, ids_ref), (hid_hbm, hid_ref),
    )
    copies = copied(pairs, sems)
    expert, tensor = lax.axis_index("expert"), lax.axis_index("tensor")
    total_rows, width = out_ref.shape
    owners = total_rows // SUB
    piece = width // CAP
    tok = hid_ref.shape[0]
    half = hid_ref.shape[1] // 2
    batch, heads, lat = ql_ref.shape
    ctx_dev = kl_ref.shape[1]

    block = SUB * tok
    row, col = iota((total_rows, block), 0), iota((total_rows, block), 1)
    kept = (row % SUB == col // tok) & (col < block - tok)
    spread = ones_where(iota((total_rows, owners), 0) // SUB == iota((total_rows, owners), 1))
    last = ones_where(
        iota((total_rows, owners), 0) == iota((total_rows, owners), 1) * SUB + (SUB - 1)
    )
    for copy in copies[:4]:
        copy.wait()
    parts = []
    for b in range(batch):
        latent = kl_ref[b]
        s = dot_nt(ql_ref[b], latent) + dot(qr_ref[b], kr_ref[b])
        valid = expert * ctx_dev + iota((heads, ctx_dev), 1) < ctx_ref[b]
        s = jnp.where(valid, s * softmax_scale, -1e30)
        top = jnp.max(s, axis=1, keepdims=True)
        p = jnp.where(valid, jnp.exp(s - top), 0.0)
        total = jnp.sum(p, axis=1, keepdims=True)
        mean = dot(p.astype(bf16), latent) / jnp.where(total > 0.0, total, 1.0)
        at = iota((heads, width - lat), 1)
        stats = jnp.zeros((heads, width - lat), f32)
        for k, number in enumerate(in_three(top) + in_three(total)):
            stats = jnp.where(at == k, number, stats)
        parts.append(jnp.concatenate([mean, stats], axis=1).astype(bf16))
    attn = jnp.concatenate(parts, axis=0)

    for copy in copies[4:]:
        copy.wait()
    _, _, match, rank = routing(ids_ref[...], owners, tok, len_ref[0])
    hidden = hid_ref[...]
    source = jnp.where(tensor == 0, hidden[:, :half], hidden[:, half:])
    stacked = [source[:, k * piece : (k + 1) * piece] for k in range(half // piece)]
    stacked.append(jnp.zeros((tok, piece), bf16))
    stacked = jnp.concatenate(stacked, axis=0)
    for c in range(CAP):
        mine = jnp.where(rank == c, match, 0.0).astype(bf16)
        lhs = jnp.where(kept, dot(spread, mine), 0.0).astype(bf16)
        at = slice(c * piece, (c + 1) * piece)
        out_ref[:, at] = (dot(lhs, stacked) + dot(last, attn[:, at])).astype(bf16)


def sort_rows(arrived, rows):
    total_rows, width = arrived.shape
    owners = total_rows // SUB
    piece = width // CAP
    row, col = iota((total_rows, total_rows), 0), iota((total_rows, total_rows), 1)
    order = ones_where(col == (row % owners) * SUB + row // owners)
    ordered = dot(order, arrived)
    for k in range(SUB - 1):
        for c in range(CAP):
            rows[c * owners : (c + 1) * owners, k * piece : (k + 1) * piece] = ordered[
                k * owners : (k + 1) * owners, c * piece : (c + 1) * piece
            ].astype(bf16)
    return ordered[(SUB - 1) * owners :]


def copied(pairs, sems):
    copies = [pltpu.make_async_copy(a, b, sems.at[k]) for k, (a, b) in enumerate(pairs)]
    for copy in copies:
        copy.start()
    return copies


def own_kernel(
    own_ref, wg_hbm, wu_hbm,
    gate_ref, upper_ref, attn_ref, next_gate_ref, next_up_ref,
    wg, wu, rows, sems,
):
    half = rows.shape[1]
    lat = attn_ref.shape[1]
    tensor = lax.axis_index("tensor")
    mine = pl.ds(pl.multiple_of(tensor * half, half), half)
    theirs = pl.ds(pl.multiple_of((1 - tensor) * half, half), half)
    copies = copied(
        (
            (wg_hbm.at[0, mine, :], wg),
            (wu_hbm.at[0, mine, :], wu),
            (wg_hbm.at[0, theirs, :], next_gate_ref),
            (wu_hbm.at[0, theirs, :], next_up_ref),
        ),
        sems,
    )
    arrived = sort_rows(own_ref[...], rows)
    stats = [arrived[:, lat + k : lat + k + 1] for k in range(6)]
    top = stats[0] + stats[1] + stats[2]
    total = stats[3] + stats[4] + stats[5]
    share = jnp.exp(top - jnp.max(top, axis=0, keepdims=True)) * total
    weighted = jnp.sum(share * arrived[:, :lat], axis=0, keepdims=True)
    done = weighted / jnp.sum(share, axis=0, keepdims=True)
    attn_ref[...] = jnp.broadcast_to(done, attn_ref.shape).astype(bf16)
    copies[0].wait()
    gate_ref[...] = dot(rows[...], wg[...])
    copies[1].wait()
    upper_ref[...] = dot(rows[...], wu[...])
    copies[2].wait()
    copies[3].wait()


def other_kernel(
    other_ref, wg_ref, wu_ref, gate_ref, upper_ref, wd_hbm,
    hidden_ref, next_down_ref,
    rows, sems,
):
    half = rows.shape[1]
    mine = pl.ds(pl.multiple_of(lax.axis_index("tensor") * half, half), half)
    copies = copied(((wd_hbm.at[0, :, mine], next_down_ref),), sems)
    sort_rows(other_ref[...], rows)
    gate = gate_ref[...] + dot(rows[...], wg_ref[...])
    upper = upper_ref[...] + dot(rows[...], wu_ref[...])
    hidden_ref[...] = (gate / (1.0 + jnp.exp(-gate)) * upper).astype(bf16)
    copies[0].wait()


def down_kernel(hidden_ref, wd_ref, sum_ref):
    sum_ref[...] = dot(hidden_ref[...], wd_ref[...])


def back_kernel(sum_ref, hidden_ref, wd_ref, attn_ref, out_ref, rows):
    total_rows, width = out_ref.shape
    owners = total_rows // SUB
    piece = width // CAP
    lat = attn_ref.shape[1]
    whole = (sum_ref[...] + dot(hidden_ref[...], wd_ref[...])).astype(bf16)
    for k in range(SUB - 1):
        for c in range(CAP):
            rows[k * owners : (k + 1) * owners, c * piece : (c + 1) * piece] = whole[
                c * owners : (c + 1) * owners, k * piece : (k + 1) * piece
            ]
    rows[(SUB - 1) * owners :, :lat] = jnp.broadcast_to(attn_ref[0:1, :], (owners, lat))
    rows[(SUB - 1) * owners :, lat:] = jnp.zeros((owners, width - lat), bf16)
    row, col = iota((total_rows, total_rows), 0), iota((total_rows, total_rows), 1)
    order = ones_where(col == (row % SUB) * owners + row // SUB)
    out_ref[...] = dot(order, rows[...]).astype(bf16)


def sum_kernel(len_ref, back_ref, ids_ref, gate_ref, moe_ref, attn_ref):
    total_rows, width = back_ref.shape
    owners = total_rows // SUB
    piece = width // CAP
    tok = ids_ref.shape[1]
    block = SUB * tok
    repeat, picks, match, rank = routing(ids_ref[...], owners, tok, len_ref[0])
    gates = gate_ref[...]
    lower = gates % 8
    split = []
    for number in (gates - lower, lower):
        number = dot(number.astype(f32).astype(bf16), repeat)
        split.append(sum(jnp.where(p, number[k : k + 1, :], 0.0) for k, p in enumerate(picks)))
    spread = ones_where(iota((owners, total_rows), 1) // SUB == iota((owners, total_rows), 0))
    row, col = iota((block, total_rows), 0), iota((block, total_rows), 1)
    kept = row // tok == col % SUB
    summed = jnp.zeros((block, piece), f32)
    for c in range(CAP):
        for number in split:
            mine = jnp.where((rank == c) & (match > 0.0), number, 0.0)
            lhs = dot(mine.T.astype(bf16), spread)
            lhs = jnp.where(kept, lhs, 0.0).astype(bf16)
            summed = summed + dot(lhs, back_ref[:, c * piece : (c + 1) * piece])
    summed = summed * (1.0 / gate_denominator)
    for k in range(SUB - 1):
        moe_ref[:, k * piece : (k + 1) * piece] = summed[k * tok : (k + 1) * tok].astype(bf16)
    lat = attn_ref.shape[1]
    last = ones_where(
        iota((owners, total_rows), 1) == iota((owners, total_rows), 0) * SUB + (SUB - 1)
    )
    attn_ref[...] = dot(last, back_ref[:, :lat]).astype(bf16)


def vmem():
    return pl.BlockSpec(memory_space=pltpu.VMEM)


def smem():
    return pl.BlockSpec(memory_space=pltpu.SMEM)


def hbm():
    return pl.BlockSpec(memory_space=pltpu.HBM)


def in_hbm(*arrays):
    return [pltpu.with_memory_space_constraint(a, pltpu.HBM) for a in arrays]


def in_vmem(*arrays):
    return [pltpu.with_memory_space_constraint(a, pltpu.VMEM) for a in arrays]


def call(kernel, out_shape, in_specs, scratch=(), vmem_mib=32):
    several = isinstance(out_shape, (tuple, list))
    return pl.pallas_call(
        kernel,
        out_shape=out_shape,
        in_specs=in_specs,
        out_specs=tuple(vmem() for _ in out_shape) if several else vmem(),
        scratch_shapes=list(scratch),
        compiler_params=pltpu.CompilerParams(vmem_limit_bytes=vmem_mib << 20),
        interpret=INTERPRET,
    )


def local(
    hidden_in,
    batch_len,
    expert_ids,
    gate_num,
    w_gate,
    w_up,
    w_down,
    q_latent,
    q_rope,
    kv_latent,
    kv_rope,
    ctx_len,
):
    owners = lax.axis_size("expert")
    tok, features = hidden_in.shape
    half = features // 2
    hidden_units = w_gate.shape[2]
    batch, heads, lat = q_latent.shape
    total_rows = owners * SUB
    slots = CAP * owners
    width = CAP * half // (SUB - 1)
    tensor = lax.axis_index("tensor")
    swap = [(0, 1), (1, 0)]

    def exchanged(packed):
        whole = packed.reshape(owners, SUB, width)
        return lax.all_to_all(whole, "expert", 0, 0, tiled=True).reshape(total_rows, width)

    ids_t, gate_t = expert_ids.T, gate_num.T
    local_arrays = (hidden_in, ids_t, q_latent, q_rope, kv_latent, kv_rope)
    packed = call(
        pack_kernel,
        jax.ShapeDtypeStruct((total_rows, width), bf16),
        [smem(), smem()] + [hbm() for _ in local_arrays],
        [pltpu.VMEM(a.shape, a.dtype) for a in local_arrays]
        + [pltpu.SemaphoreType.DMA((len(local_arrays),))],
    )(batch_len, ctx_len, *in_hbm(*local_arrays))
    own = exchanged(packed)
    given = lax.dynamic_slice_in_dim(w_down[0], (1 - tensor) * half, half, 1)
    down_other = lax.ppermute(given, "tensor", swap)
    other = lax.ppermute(own, "tensor", swap)
    partial = jax.ShapeDtypeStruct((slots, hidden_units), f32)
    half_weights = pltpu.VMEM((half, hidden_units), bf16)
    gate, upper, attn, next_gate, next_up = call(
        own_kernel,
        (partial, partial, jax.ShapeDtypeStruct((16, lat), bf16), half_weights, half_weights),
        [vmem(), hbm(), hbm()],
        [
            half_weights,
            half_weights,
            pltpu.VMEM((slots, half), bf16),
            pltpu.SemaphoreType.DMA((4,)),
        ],
    )(own, *in_hbm(w_gate, w_up))
    hidden, next_down = call(
        other_kernel,
        (
            jax.ShapeDtypeStruct((slots, hidden_units), bf16),
            pltpu.VMEM((hidden_units, half), bf16),
        ),
        [vmem() for _ in range(5)] + [hbm()],
        [pltpu.VMEM((slots, half), bf16), pltpu.SemaphoreType.DMA((1,))],
    )(other, *in_vmem(next_gate, next_up), gate, upper, *in_hbm(w_down))
    hidden_other = lax.ppermute(hidden, "tensor", swap)
    summed = call(down_kernel, jax.ShapeDtypeStruct((slots, half), f32), [vmem(), vmem()])(
        hidden, *in_vmem(next_down)
    )
    returned = call(
        back_kernel,
        jax.ShapeDtypeStruct((total_rows, width), bf16),
        [vmem() for _ in range(4)],
        [pltpu.VMEM((total_rows, width), bf16)],
    )(summed, hidden_other, down_other, attn)
    back = exchanged(returned)
    moe_half, attn_out = call(
        sum_kernel,
        (
            jax.ShapeDtypeStruct((tok, half), bf16),
            jax.ShapeDtypeStruct((batch * heads, lat), bf16),
        ),
        [smem(), vmem(), vmem(), vmem()],
    )(batch_len, back, ids_t, gate_t)
    moe_other = lax.ppermute(moe_half, "tensor", swap)
    moe_out = jnp.where(
        tensor == 0,
        jnp.concatenate([moe_half, moe_other], axis=1),
        jnp.concatenate([moe_other, moe_half], axis=1),
    )
    return moe_out, attn_out.reshape(batch, heads, lat)


def solution(mesh):
    both = ("groups", "expert")
    in_specs = (
        P(both, None),
        P("groups"),
        P(both, None),
        P(both, None),
        P("expert", None, "tensor"),
        P("expert", None, "tensor"),
        P("expert", "tensor", None),
        P("groups", "tensor", None),
        P("groups", "tensor", None),
        P("groups", "expert", None),
        P("groups", None, "expert"),
        P("groups"),
    )
    out_specs = (P(both, None), P("groups", "tensor", None))
    return jax.shard_map(local, mesh=mesh, in_specs=in_specs, out_specs=out_specs, check_vma=False)
```

time: 102 us -> 94.1 us (0.923)
  starting transfers between devices: 17.1 us -> 37.1 us
  waiting for transfers between devices: 26.5 us -> 10.7 us
  blocking collectives: 38.9 us -> 27.9 us
  local copies, waits for them, and re-layouts: 5.65 us -> 3.53 us
    all_to_all x1, starting transfers between devices: 7.11 us -> 21.8 us  [exchanged(): lax.all_to_all(whole, 'expert', 0, 0, tiled=True).reshape(total_rows, width)]
    all_to_all x1, waiting for transfers between devices: 20.9 us -> 8.93 us  [exchanged(): lax.all_to_all(whole, 'expert', 0, 0, tiled=True).reshape(total_rows, width)]
    all_to_all x1, blocking collectives: 38.9 us -> 27.9 us  [exchanged(): lax.all_to_all(whole, 'expert', 0, 0, tiled=True).reshape(total_rows, width)]
    unnamed x16 -> x6, local copies, waits for them, and re-layouts: 5.65 us -> 0.66 us
    ppermute x1 -> x2, starting transfers between devices: 0.49 us -> 5.25 us  [the longest x1 5.11 us: local(): down_other = lax.ppermute(given, 'tensor', swap)]
    dynamic_slice x0 -> x1, local copies, waits for them, and re-layouts: none -> 2.88 us  [local(): given = lax.dynamic_slice_in_dim(w_down[0], (1 - tensor) * half, half, 1)]
    pallas_call x1, Pallas kernels: 1.82 us -> 4.07 us  [local(): call(pack_kernel, jax.ShapeDtypeStruct((total_rows, width), bf16), [smem(...]
    ppermute x1, waiting for transfers between devices: 1.91 us -> 0.01 us  [local(): other = lax.ppermute(own, 'tensor', swap)]
  transfers between devices with their start and end apart: 4 -> 5, of which waited for: 4 -> 3; matrix products, arithmetic and copies ran while one was open for 0% -> 3% of each run, Pallas kernels for 0% -> 6%
where the time goes in v2:
time: 94.1 us; the launch traced here: 93.8 us
  starting transfers between devices  37.1 us (39%)
  blocking collectives  27.9 us (30%)
  Pallas kernels  12.5 us (13%)
  waiting for transfers between devices  10.7 us (11%)
  local copies, waits for them, and re-layouts  3.53 us (4%)
  between operations  1.36 us (1%)
    all_to_all x1, blocking collectives, exchanged(): lax.all_to_all(whole, 'expert', 0, 0, tiled=True).reshape(total_rows, width)  27.9 us
    all_to_all x1, starting transfers between devices, exchanged(): lax.all_to_all(whole, 'expert', 0, 0, tiled=True).reshape(total_rows, width)  21.8 us
    all_to_all x1, waiting for transfers between devices, exchanged(): lax.all_to_all(whole, 'expert', 0, 0, tiled=True).reshape(total_rows, width)  8.93 us
    ppermute x1, starting transfers between devices, local(): other = lax.ppermute(own, 'tensor', swap)  7.43 us
    ppermute x1, starting transfers between devices, local(): down_other = lax.ppermute(given, 'tensor', swap)  5.11 us
    pallas_call x1, Pallas kernels, local(): call(pack_kernel, jax.ShapeDtypeStruct((total_rows, width), bf16), [smem(...  4.07 us
    pallas_call x1, Pallas kernels, local(): call(own_kernel, (partial, partial, jax.ShapeDtypeStruct((16, lat), bf16)...  3.37 us
    dynamic_slice x1, local copies, waits for them, and re-layouts, local(): given = lax.dynamic_slice_in_dim(w_down[0], (1 - tensor) * half, half, 1)  2.88 us
  transfers between devices with their start and end apart: 5, of which 3 were waited for; matrix products, arithmetic and copies ran while one was open for 3% of the time, Pallas kernels for 6%

profile of v2, /device:TPU:513, one launch (start us, length us, event | category | flops | bytes accessed | tf_op | source)
XLA Modules:
  0.0 93.8 jit_solution(7939337483893662162)
XLA Ops:
  1.3 0.0 copy-start.2
  1.3 0.6 copy-done.2
  1.9 4.1 %shard_map.131 = bf16[512,768]{1,0:T(8,128)(2,1)} custom-call(s32[1]{0:T(128)S(6)} %copy.14.len_ref, s32[2]{0:T(128)S(1)} %copy-done.2, bf16[16,3584]{1,0:T(8,128)(2,1)} %hid_hbm.1, s32[8,16]{1,0:T(8,128)} %bitcast.13, bf16[2,32,512]{2,1,0:T(8,128)(2,1)} %ql_hbm.1, bf16[2,32,64]{2,1,0:T(8,128)(2,1)} %qr_hbm.1, bf16[2,128,512]{2,1,0:T(8,128)(2,1)} %kl_hbm.1, ...), custom_call_target="tpu_custom_call" | custom-call | tf_op jit(solution)/shard_map/pallas_call | solution.py:307
  6.0 21.8 %all-to-all-start = ((bf16[64,8,768]{2,1,0:T(8,128)(2,1)}), bf16[64,8,768]{2,1,0:T(8,128)(2,1)S(1)}, u32[]{:S(2)}, u32[]{:S(2)}) async-start(bf16[64,8,768]{2,1,0:T(8,128)(2,1)} %bitcast.1), calls=%async_computation | async-start | bytes 1572864 | tf_op jit(solution)/shard_map/all_to_all | solution.py:303
  27.8 2.9 %dynamic-slice_bitcast_fusion = bf16[512,1792]{1,0:T(8,128)(2,1)} fusion(bf16[1,512,3584]{2,1,0:T(8,128)(2,1)} %wd_hbm.1, s32[]{:T(128)S(6)} %select_n.12), kind=kLoop, calls=%fused_computation | loop fusion | bytes 3670020 | tf_op jit(solution)/shard_map/dynamic_slice | solution.py:315
  30.7 5.1 %collective-permute-start.2 = (bf16[512,1792]{1,0:T(8,128)(2,1)}, bf16[512,1792]{1,0:T(8,128)(2,1)S(1)}, u32[]{:S(2)}, u32[]{:S(2)}) collective-permute-start(bf16[512,1792]{1,0:T(8,128)(2,1)} %dynamic-slice_bitcast_fusion), channel_id=1, source_target_pairs={{0,1},{1,0},{2,3},{3,2},{4,5},{5,4},{6,7},{7,6},{8,9},{9,8},{10,11... | collective-permute-start | bytes 5505032 | tf_op jit(solution)/shard_map/ppermute | solution.py:316
  35.8 8.9 %all-to-all-done = bf16[64,8,768]{2,1,0:T(8,128)(2,1)S(1)} async-done(((bf16[64,8,768]{2,1,0:T(8,128)(2,1)}), bf16[64,8,768]{2,1,0:T(8,128)(2,1)S(1)}, u32[]{:S(2)}, u32[]{:S(2)}) %all-to-all-start) | async-done | bytes 786464 | tf_op jit(solution)/shard_map/all_to_all | solution.py:303
  44.8 7.4 %collective-permute-start = (bf16[512,768]{1,0:T(8,128)(2,1)S(1)}, bf16[512,768]{1,0:T(8,128)(2,1)S(1)}, u32[]{:S(2)}, u32[]{:S(2)}) collective-permute-start(bf16[512,768]{1,0:T(8,128)(2,1)S(1)} %bitcast.11), channel_id=1, source_target_pairs={{0,1},{1,0},{2,3},{3,2},{4,5},{5,4},{6,7},{7,6},{8,9},{9,8},{10,11... | collective-permute-start | bytes 2359304 | tf_op jit(solution)/shard_map/ppermute | solution.py:317
  52.2 3.4 %shard_map.132 = (f32[192,512]{1,0:T(8,128)S(1)}, f32[192,512]{1,0:T(8,128)S(1)}, bf16[16,512]{1,0:T(8,128)(2,1)S(1)}, bf16[1792,512]{1,0:T(8,128)(2,1)S(1)}, bf16[1792,512]{1,0:T(8,128)(2,1)S(1)}) custom-call(bf16[512,768]{1,0:T(8,128)(2,1)S(1)} %bitcast.12, bf16[1,3584,512]{2,1,0:T(8,128)(2,1)} %wg_hbm.1, bf16[1,3584,512]{2,1,0:T(8,128)(2,1)} %wu_hbm.1), custom_call_target="tpu_custom_call" | custom-call | tf_op jit(solution)/shard_map/pallas_call | solution.py:320
  55.6 0.0 collective-permute-done.other_ref
  55.6 1.8 %shard_map.133 = (bf16[192,512]{1,0:T(8,128)(2,1)S(1)}, bf16[512,1792]{1,0:T(8,128)(2,1)S(1)}) custom-call(bf16[512,768]{1,0:T(8,128)(2,1)S(1)} %collective-permute-done.other_ref, bf16[1792,512]{1,0:T(8,128)(2,1)S(1)} %get-tuple-element.11.wg_ref, bf16[1792,512]{1,0:T(8,128)(2,1)S(1)} %get-tuple-element.12.wu_ref, ...), custom_call_target="tpu_custom_call" | custom-call | tf_op jit(solution)/shard_map/pallas_call | solution.py:331
  57.4 0.1 collective-permute-start.1
  57.5 0.5 shard_map.134.sum_ref
  58.0 0.0 collective-permute-done.2.wd_ref
  58.1 0.9 collective-permute-done.1.hidden_ref
  58.9 0.0 copy-start
  58.9 0.0 copy-start.1
  58.9 1.1 %shard_map.135 = bf16[512,768]{1,0:T(8,128)(2,1)S(1)} custom-call(f32[192,1792]{1,0:T(8,128)S(1)} %shard_map.134.sum_ref, bf16[192,512]{1,0:T(8,128)(2,1)S(1)} %collective-permute-done.1.hidden_ref, bf16[512,1792]{1,0:T(8,128)(2,1)S(1)} %collective-permute-done.2.wd_ref, bf16[16,512]{1,0:T(8,128)(2,1)S(1)} %get-tuple-element.17.attn_ref), custom_call_target="tpu_custom_call" | custom-call | tf_op jit(solution)/shard_map/pallas_call | solution.py:344
  60.1 27.9 %all_to_all.10 = bf16[64,8,768]{2,1,0:T(8,128)(2,1)S(1)} all-to-all(bf16[64,8,768]{2,1,0:T(8,128)(2,1)S(1)} %bitcast.9), channel_id=1, replica_groups=mesh['groups'=2,'expert'=64,'tensor'=2] {'expert'}, dimensions={0} | all-to-all | bytes 1572864 | tf_op jit(solution)/shard_map/all_to_all | solution.py:303
  88.0 0.0 copy-done
  88.0 0.0 copy-done.1
  88.0 1.6 %shard_map.136 = (bf16[16,1792]{1,0:T(8,128)(2,1)S(1)}, bf16[64,512]{1,0:T(8,128)(2,1)}) custom-call(s32[1]{0:T(128)S(6)} %copy.14.len_ref, bf16[512,768]{1,0:T(8,128)(2,1)S(1)} %bitcast.10, s32[8,16]{1,0:T(8,128)S(1)} %bitcast.14, s32[8,16]{1,0:T(8,128)S(1)} %bitcast.15), custom_call_target="tpu_custom_call" | custom-call | tf_op jit(solution)/shard_map/pallas_call | solution.py:351
  89.6 2.6 %collective-permute-start.3 = (bf16[16,1792]{1,0:T(8,128)(2,1)S(1)}, bf16[16,1792]{1,0:T(8,128)(2,1)S(1)}, u32[]{:S(2)}, u32[]{:S(2)}) collective-permute-start(bf16[16,1792]{1,0:T(8,128)(2,1)S(1)} %get-tuple-element.18), channel_id=1, source_target_pairs={{0,1},{1,0},{2,3},{3,2},{4,5},{5,4},{6,7},{7,6},{8,9},{9,8},{10,11... | collective-permute-start | bytes 172040 | tf_op jit(solution)/shard_map/ppermute | solution.py:359
  92.2 0.9 collective-permute-done.3
  93.1 0.7 maximum_select_fusion
Async XLA Ops:
  1.3 0.7 copy-start.2
  6.0 38.8 %all-to-all-start = ((bf16[64,8,768]{2,1,0:T(8,128)(2,1)}), bf16[64,8,768]{2,1,0:T(8,128)(2,1)S(1)}, u32[]{:S(2)}, u32[]{:S(2)}) async-start(bf16[64,8,768]{2,1,0:T(8,128)(2,1)} %bitcast.1), calls=%async_computation | async-start | bytes 1572864 | tf_op jit(solution)/shard_map/all_to_all | solution.py:303
  30.7 27.3 %collective-permute-start.2 = (bf16[512,1792]{1,0:T(8,128)(2,1)}, bf16[512,1792]{1,0:T(8,128)(2,1)S(1)}, u32[]{:S(2)}, u32[]{:S(2)}) collective-permute-start(bf16[512,1792]{1,0:T(8,128)(2,1)} %dynamic-slice_bitcast_fusion), channel_id=1, source_target_pairs={{0,1},{1,0},{2,3},{3,2},{4,5},{5,4},{6,7},{7,6},{8,9},{9,8},{10,11... | collective-permute-start | bytes 5505032 | tf_op jit(solution)/shard_map/ppermute | solution.py:316
  44.8 10.8 %collective-permute-start = (bf16[512,768]{1,0:T(8,128)(2,1)S(1)}, bf16[512,768]{1,0:T(8,128)(2,1)S(1)}, u32[]{:S(2)}, u32[]{:S(2)}) collective-permute-start(bf16[512,768]{1,0:T(8,128)(2,1)S(1)} %bitcast.11), channel_id=1, source_target_pairs={{0,1},{1,0},{2,3},{3,2},{4,5},{5,4},{6,7},{7,6},{8,9},{9,8},{10,11... | collective-permute-start | bytes 2359304 | tf_op jit(solution)/shard_map/ppermute | solution.py:317
  57.4 1.6 %collective-permute-start.1 = (bf16[192,512]{1,0:T(8,128)(2,1)S(1)}, bf16[192,512]{1,0:T(8,128)(2,1)S(1)}, u32[]{:S(2)}, u32[]{:S(2)}) collective-permute-start(bf16[192,512]{1,0:T(8,128)(2,1)S(1)} %get-tuple-element.15.hidden_ref), channel_id=1, source_target_pairs={{0,1},{1,0},{2,3},{3,2},{4,5},{5,4},{6,7},{7,6},{8,9},{9,8},{10,11... | collective-permute-start | bytes 589832 | tf_op jit(solution)/shard_map/ppermute | solution.py:340
  58.9 29.1 %copy-start = (s32[16,8]{0,1:T(8,128)S(1)}, s32[16,8]{0,1:T(8,128)}, u32[]{:S(2)}) copy-start(s32[16,8]{0,1:T(8,128)} %param.14) | copy-start | bytes 1540
  58.9 29.1 %copy-start.1 = (s32[16,8]{0,1:T(8,128)S(1)}, s32[16,8]{0,1:T(8,128)}, u32[]{:S(2)}) copy-start(s32[16,8]{0,1:T(8,128)} %param.15) | copy-start | bytes 1540
  89.6 3.5 %collective-permute-start.3 = (bf16[16,1792]{1,0:T(8,128)(2,1)S(1)}, bf16[16,1792]{1,0:T(8,128)(2,1)S(1)}, u32[]{:S(2)}, u32[]{:S(2)}) collective-permute-start(bf16[16,1792]{1,0:T(8,128)(2,1)S(1)} %get-tuple-element.18), channel_id=1, source_target_pairs={{0,1},{1,0},{2,3},{3,2},{4,5},{5,4},{6,7},{7,6},{8,9},{9,8},{10,11... | collective-permute-start | bytes 172040 | tf_op jit(solution)/shard_map/ppermute | solution.py:359

commit v3 on v2

--- a/solution.py
+++ b/solution.py
@@ -1,5 +1,3 @@
-import functools
-
 import jax
 import jax.numpy as jnp
 from jax import lax
@@ -13,7 +11,7 @@
 f32 = jnp.float32
 softmax_scale = 192.0 ** (-0.5)
 gate_denominator = 1024.0
-INTERPRET = False
+BLOCKS = 2
 
 
 def iota(shape, dim):
@@ -54,13 +52,13 @@
 
 
 def pack_kernel(
-    len_ref, ctx_ref, hid_hbm, ids_hbm, ql_hbm, qr_hbm, kl_hbm, kr_hbm,
+    len_ref, ctx_hbm, hid_hbm, ids_hbm, ql_hbm, qr_hbm, kl_hbm, kr_hbm,
     out_ref,
-    hid_ref, ids_ref, ql_ref, qr_ref, kl_ref, kr_ref, sems,
+    ctx_ref, hid_ref, ids_ref, ql_ref, qr_ref, kl_ref, kr_ref, sems,
 ):
     pairs = (
-        (ql_hbm, ql_ref), (kl_hbm, kl_ref), (qr_hbm, qr_ref),
-        (kr_hbm, kr_ref), (ids_hbm, ids_ref), (hid_hbm, hid_ref),
+        (ql_hbm, ql_ref), (kl_hbm, kl_ref), (qr_hbm, qr_ref), (kr_hbm, kr_ref), (ctx_hbm, ctx_ref),
+        (ids_hbm, ids_ref), (hid_hbm, hid_ref),
     )
     copies = copied(pairs, sems)
     expert, tensor = lax.axis_index("expert"), lax.axis_index("tensor")
@@ -79,7 +77,7 @@
     last = ones_where(
         iota((total_rows, owners), 0) == iota((total_rows, owners), 1) * SUB + (SUB - 1)
     )
-    for copy in copies[:4]:
+    for copy in copies[:5]:
         copy.wait()
     parts = []
     for b in range(batch):
@@ -98,7 +96,7 @@
         parts.append(jnp.concatenate([mean, stats], axis=1).astype(bf16))
     attn = jnp.concatenate(parts, axis=0)
 
-    for copy in copies[4:]:
+    for copy in copies[5:]:
         copy.wait()
     _, _, match, rank = routing(ids_ref[...], owners, tok, len_ref[0])
     hidden = hid_ref[...]
@@ -117,15 +115,21 @@
     total_rows, width = arrived.shape
     owners = total_rows // SUB
     piece = width // CAP
-    row, col = iota((total_rows, total_rows), 0), iota((total_rows, total_rows), 1)
-    order = ones_where(col == (row % owners) * SUB + row // owners)
-    ordered = dot(order, arrived)
-    for k in range(SUB - 1):
-        for c in range(CAP):
-            rows[c * owners : (c + 1) * owners, k * piece : (k + 1) * piece] = ordered[
-                k * owners : (k + 1) * owners, c * piece : (c + 1) * piece
-            ].astype(bf16)
-    return ordered[(SUB - 1) * owners :]
+    part = owners // BLOCKS
+    size = SUB * part
+    row, col = iota((size, size), 0), iota((size, size), 1)
+    order = ones_where(col == (row % part) * SUB + row // part)
+    attention = []
+    for b in range(BLOCKS):
+        ordered = dot(order, arrived[b * size : (b + 1) * size])
+        for k in range(SUB - 1):
+            for c in range(CAP):
+                first = c * owners + b * part
+                rows[first : first + part, k * piece : (k + 1) * piece] = ordered[
+                    k * part : (k + 1) * part, c * piece : (c + 1) * piece
+                ].astype(bf16)
+        attention.append(ordered[size - part :])
+    return jnp.concatenate(attention, axis=0)
 
 
 def copied(pairs, sems):
@@ -185,8 +189,9 @@
     copies[0].wait()
 
 
-def down_kernel(hidden_ref, wd_ref, sum_ref):
+def down_kernel(hidden_ref, wd_ref, len_ref, ids_ref, gate_ref, sum_ref, weigh_ref):
     sum_ref[...] = dot(hidden_ref[...], wd_ref[...])
+    weigh(len_ref, ids_ref, gate_ref, weigh_ref)
 
 
 def back_kernel(sum_ref, hidden_ref, wd_ref, attn_ref, out_ref, rows):
@@ -194,25 +199,28 @@
     owners = total_rows // SUB
     piece = width // CAP
     lat = attn_ref.shape[1]
-    whole = (sum_ref[...] + dot(hidden_ref[...], wd_ref[...])).astype(bf16)
-    for k in range(SUB - 1):
-        for c in range(CAP):
-            rows[k * owners : (k + 1) * owners, c * piece : (c + 1) * piece] = whole[
-                c * owners : (c + 1) * owners, k * piece : (k + 1) * piece
-            ]
-    rows[(SUB - 1) * owners :, :lat] = jnp.broadcast_to(attn_ref[0:1, :], (owners, lat))
-    rows[(SUB - 1) * owners :, lat:] = jnp.zeros((owners, width - lat), bf16)
-    row, col = iota((total_rows, total_rows), 0), iota((total_rows, total_rows), 1)
-    order = ones_where(col == (row % SUB) * owners + row // SUB)
-    out_ref[...] = dot(order, rows[...]).astype(bf16)
-
-
-def sum_kernel(len_ref, back_ref, ids_ref, gate_ref, moe_ref, attn_ref):
-    total_rows, width = back_ref.shape
+    mine = pl.ds(pl.multiple_of(lax.axis_index("tensor") * sum_ref.shape[1], sum_ref.shape[1]), sum_ref.shape[1])
+    whole = (sum_ref[...] + dot(hidden_ref[...], wd_ref[0, :, mine])).astype(bf16)
+    part = owners // BLOCKS
+    size = SUB * part
+    row, col = iota((size, size), 0), iota((size, size), 1)
+    order = ones_where(col == (row % SUB) * part + row // SUB)
+    rows[size - part :, :lat] = jnp.broadcast_to(attn_ref[0:1, :], (part, lat))
+    rows[size - part :, lat:] = jnp.zeros((part, width - lat), bf16)
+    for b in range(BLOCKS):
+        for k in range(SUB - 1):
+            for c in range(CAP):
+                first = c * owners + b * part
+                rows[k * part : (k + 1) * part, c * piece : (c + 1) * piece] = whole[
+                    first : first + part, k * piece : (k + 1) * piece
+                ]
+        out_ref[b * size : (b + 1) * size, :] = dot(order, rows[...]).astype(bf16)
+
+
+def weigh(len_ref, ids_ref, gate_ref, weigh_ref):
+    tok = ids_ref.shape[1]
+    block, total_rows = SUB * tok, weigh_ref.shape[2]
     owners = total_rows // SUB
-    piece = width // CAP
-    tok = ids_ref.shape[1]
-    block = SUB * tok
     repeat, picks, match, rank = routing(ids_ref[...], owners, tok, len_ref[0])
     gates = gate_ref[...]
     lower = gates % 8
@@ -223,14 +231,22 @@
     spread = ones_where(iota((owners, total_rows), 1) // SUB == iota((owners, total_rows), 0))
     row, col = iota((block, total_rows), 0), iota((block, total_rows), 1)
     kept = row // tok == col % SUB
-    summed = jnp.zeros((block, piece), f32)
     for c in range(CAP):
-        for number in split:
+        for n, number in enumerate(split):
             mine = jnp.where((rank == c) & (match > 0.0), number, 0.0)
-            lhs = dot(mine.T.astype(bf16), spread)
-            lhs = jnp.where(kept, lhs, 0.0).astype(bf16)
-            summed = summed + dot(lhs, back_ref[:, c * piece : (c + 1) * piece])
-    summed = summed * (1.0 / gate_denominator)
+            weigh_ref[2 * c + n] = jnp.where(kept, dot(mine.T.astype(bf16), spread), 0.0).astype(bf16)
+
+
+def sum_kernel(weigh_ref, back_ref, moe_ref, attn_ref):
+    total_rows, width = back_ref.shape
+    owners = total_rows // SUB
+    piece = width // CAP
+    tok, _ = moe_ref.shape
+    summed = sum(
+        dot(weigh_ref[2 * c + n], back_ref[:, c * piece : (c + 1) * piece])
+        for c in range(CAP)
+        for n in range(2)
+    ) * (1.0 / gate_denominator)
     for k in range(SUB - 1):
         moe_ref[:, k * piece : (k + 1) * piece] = summed[k * tok : (k + 1) * tok].astype(bf16)
     lat = attn_ref.shape[1]
@@ -269,7 +285,6 @@
         out_specs=tuple(vmem() for _ in out_shape) if several else vmem(),
         scratch_shapes=list(scratch),
         compiler_params=pltpu.CompilerParams(vmem_limit_bytes=vmem_mib << 20),
-        interpret=INTERPRET,
     )
 
 
@@ -303,18 +318,18 @@
         return lax.all_to_all(whole, "expert", 0, 0, tiled=True).reshape(total_rows, width)
 
     ids_t, gate_t = expert_ids.T, gate_num.T
-    local_arrays = (hidden_in, ids_t, q_latent, q_rope, kv_latent, kv_rope)
+    arrays = (hidden_in, ids_t, q_latent, q_rope, kv_latent, kv_rope)
     packed = call(
         pack_kernel,
-        jax.ShapeDtypeStruct((total_rows, width), bf16),
-        [smem(), smem()] + [hbm() for _ in local_arrays],
-        [pltpu.VMEM(a.shape, a.dtype) for a in local_arrays]
-        + [pltpu.SemaphoreType.DMA((len(local_arrays),))],
-    )(batch_len, ctx_len, *in_hbm(*local_arrays))
+        pltpu.VMEM((total_rows, width), bf16),
+        [smem()] + [hbm() for _ in range(7)],
+        [pltpu.SMEM(ctx_len.shape, ctx_len.dtype)]
+        + [pltpu.VMEM(a.shape, a.dtype) for a in arrays]
+        + [pltpu.SemaphoreType.DMA((7,))],
+    )(batch_len, *in_hbm(ctx_len, *arrays))
     own = exchanged(packed)
-    given = lax.dynamic_slice_in_dim(w_down[0], (1 - tensor) * half, half, 1)
-    down_other = lax.ppermute(given, "tensor", swap)
     other = lax.ppermute(own, "tensor", swap)
+    down_other = lax.ppermute(w_down, "tensor", swap)
     partial = jax.ShapeDtypeStruct((slots, hidden_units), f32)
     half_weights = pltpu.VMEM((half, hidden_units), bf16)
     gate, upper, attn, next_gate, next_up = call(
@@ -338,15 +353,20 @@
         [pltpu.VMEM((slots, half), bf16), pltpu.SemaphoreType.DMA((1,))],
     )(other, *in_vmem(next_gate, next_up), gate, upper, *in_hbm(w_down))
     hidden_other = lax.ppermute(hidden, "tensor", swap)
-    summed = call(down_kernel, jax.ShapeDtypeStruct((slots, half), f32), [vmem(), vmem()])(
-        hidden, *in_vmem(next_down)
-    )
+    summed, weights = call(
+        down_kernel,
+        (
+            jax.ShapeDtypeStruct((slots, half), f32),
+            jax.ShapeDtypeStruct((2 * CAP, SUB * tok, total_rows), bf16),
+        ),
+        [vmem(), vmem(), smem(), vmem(), vmem()],
+    )(hidden, *in_vmem(next_down), batch_len, ids_t, gate_t)
     returned = call(
         back_kernel,
         jax.ShapeDtypeStruct((total_rows, width), bf16),
         [vmem() for _ in range(4)],
-        [pltpu.VMEM((total_rows, width), bf16)],
-    )(summed, hidden_other, down_other, attn)
+        [pltpu.VMEM((total_rows // BLOCKS, width), bf16)],
+    )(summed, hidden_other, *in_vmem(down_other), attn)
     back = exchanged(returned)
     moe_half, attn_out = call(
         sum_kernel,
@@ -354,8 +374,8 @@
             jax.ShapeDtypeStruct((tok, half), bf16),
             jax.ShapeDtypeStruct((batch * heads, lat), bf16),
         ),
-        [smem(), vmem(), vmem(), vmem()],
-    )(batch_len, back, ids_t, gate_t)
+        [vmem(), vmem()],
+    )(weights, back)
     moe_other = lax.ppermute(moe_half, "tensor", swap)
     moe_out = jnp.where(
         tensor == 0,

time: 94.1 us -> 95.8 us (1.018)
  blocking collectives: 27.9 us -> 56.3 us
  starting transfers between devices: 37.1 us -> 25.1 us
  waiting for transfers between devices: 10.7 us -> 1.19 us
  local copies, waits for them, and re-layouts: 3.53 us -> 0.01 us
  Pallas kernels: 12.5 us -> 10.9 us
    all_to_all x1 -> x2, blocking collectives: 27.9 us -> 56.3 us  [exchanged(): lax.all_to_all(whole, 'expert', 0, 0, tiled=True).reshape(total_rows, width)]
    all_to_all x1 -> x0, starting transfers between devices: 21.8 us -> none  [exchanged(): lax.all_to_all(whole, 'expert', 0, 0, tiled=True).reshape(total_rows, width)]
    ppermute x1, starting transfers between devices: 5.11 us -> 20.5 us  [local(): down_other = lax.ppermute(w_down, 'tensor', swap)]
    all_to_all x1 -> x0, waiting for transfers between devices: 8.93 us -> none  [exchanged(): lax.all_to_all(whole, 'expert', 0, 0, tiled=True).reshape(total_rows, width)]
    ppermute x1, starting transfers between devices: 7.43 us -> 1.85 us  [local(): other = lax.ppermute(own, 'tensor', swap)]
    dynamic_slice x1 -> x0, local copies, waits for them, and re-layouts: 2.88 us -> none  [local(): given = lax.dynamic_slice_in_dim(w_down[0], (1 - tensor) * half, half, 1)]
  transfers between devices with their start and end apart: 5 -> 4, of which waited for: 3 -> 2; matrix products, arithmetic and copies ran while one was open for 3% -> 0% of each run, Pallas kernels for 6% -> 9%
where the time goes in v3:
time: 95.8 us; the launch traced here: 95.5 us
  blocking collectives  56.3 us (59%)
  starting transfers between devices  25.1 us (26%)
  Pallas kernels  10.9 us (11%)
  between operations  1.37 us (1%)
  waiting for transfers between devices  1.19 us (1%)
    all_to_all x2, blocking collectives, exchanged(): lax.all_to_all(whole, 'expert', 0, 0, tiled=True).reshape(total_rows, width)  56.3 us
    ppermute x1, starting transfers between devices, local(): down_other = lax.ppermute(w_down, 'tensor', swap)  20.5 us
    pallas_call x1, Pallas kernels, local(): call(own_kernel, (partial, partial, jax.ShapeDtypeStruct((16, lat), bf16)...  3.58 us
    pallas_call x1, Pallas kernels, local(): call(pack_kernel, pltpu.VMEM((total_rows, width), bf16), [smem()] + [hbm(...  2.66 us
    ppermute x1, starting transfers between devices, local(): moe_other = lax.ppermute(moe_half, 'tensor', swap)  2.54 us
  transfers between devices with their start and end apart: 4, of which 2 were waited for; matrix products, arithmetic and copies ran while one was open for 0% of the time, Pallas kernels for 9%

profile of v3, /device:TPU:513, one launch (start us, length us, event | category | flops | bytes accessed | tf_op | source)
XLA Modules:
  0.0 95.5 jit_solution(17074961531939905019)
XLA Ops:
  0.6 20.5 %collective-permute-start.2 = (bf16[1,512,3584]{2,1,0:T(8,128)(2,1)}, bf16[1,512,3584]{2,1,0:T(8,128)(2,1)S(1)}, u32[]{:S(2)}, u32[]{:S(2)}) collective-permute-start(bf16[1,512,3584]{2,1,0:T(8,128)(2,1)} %wd_hbm.1), channel_id=1, source_target_pairs={{0,1},{1,0},{2,3},{3,2},{4,5},{5,4},{6,7},{7,6},{8,9},{9,8},{10,11... | collective-permute-start | bytes 11010056 | tf_op jit(solution)/shard_map/ppermute | solution.py:332
  21.8 2.7 %shard_map.131 = bf16[512,768]{1,0:T(8,128)(2,1)S(1)} custom-call(s32[1]{0:T(128)S(6)} %copy.14.len_ref, s32[2]{0:T(128)} %ctx_hbm.1, bf16[16,3584]{1,0:T(8,128)(2,1)} %hid_hbm.1, s32[8,16]{1,0:T(8,128)} %bitcast.12, bf16[2,32,512]{2,1,0:T(8,128)(2,1)} %ql_hbm.1, bf16[2,32,64]{2,1,0:T(8,128)(2,1)} %qr_hbm.1, bf16[2,128,512]{2,1,0:T(8,128)(2,1)} %kl_hbm.1, ...), custom_call_target="tpu_custom_call" | custom-call | tf_op jit(solution)/shard_map/pallas_call | solution.py:322
  24.5 27.5 %all_to_all.10 = bf16[64,8,768]{2,1,0:T(8,128)(2,1)S(1)} all-to-all(bf16[64,8,768]{2,1,0:T(8,128)(2,1)S(1)} %bitcast.8), channel_id=1, replica_groups=mesh['groups'=2,'expert'=64,'tensor'=2] {'expert'}, dimensions={0} | all-to-all | bytes 1572864 | tf_op jit(solution)/shard_map/all_to_all | solution.py:318
  52.0 1.9 %collective-permute-start = (bf16[512,768]{1,0:T(8,128)(2,1)S(1)}, bf16[512,768]{1,0:T(8,128)(2,1)S(1)}, u32[]{:S(2)}, u32[]{:S(2)}) collective-permute-start(bf16[512,768]{1,0:T(8,128)(2,1)S(1)} %bitcast.10), channel_id=1, source_target_pairs={{0,1},{1,0},{2,3},{3,2},{4,5},{5,4},{6,7},{7,6},{8,9},{9,8},{10,11... | collective-permute-start | bytes 2359304 | tf_op jit(solution)/shard_map/ppermute | solution.py:331
  53.8 3.6 %shard_map.132 = (f32[192,512]{1,0:T(8,128)S(1)}, f32[192,512]{1,0:T(8,128)S(1)}, bf16[16,512]{1,0:T(8,128)(2,1)S(1)}, bf16[1792,512]{1,0:T(8,128)(2,1)S(1)}, bf16[1792,512]{1,0:T(8,128)(2,1)S(1)}) custom-call(bf16[512,768]{1,0:T(8,128)(2,1)S(1)} %bitcast.11, bf16[1,3584,512]{2,1,0:T(8,128)(2,1)} %wg_hbm.1, bf16[1,3584,512]{2,1,0:T(8,128)(2,1)} %wu_hbm.1), custom_call_target="tpu_custom_call" | custom-call | tf_op jit(solution)/shard_map/pallas_call | solution.py:335
  57.4 0.0 collective-permute-done.other_ref
  57.5 0.0 copy-start
  57.5 0.0 copy-start.1
  57.5 1.5 %shard_map.133 = (bf16[192,512]{1,0:T(8,128)(2,1)S(1)}, bf16[512,1792]{1,0:T(8,128)(2,1)S(1)}) custom-call(bf16[512,768]{1,0:T(8,128)(2,1)S(1)} %collective-permute-done.other_ref, bf16[1792,512]{1,0:T(8,128)(2,1)S(1)} %get-tuple-element.13.wg_ref, bf16[1792,512]{1,0:T(8,128)(2,1)S(1)} %get-tuple-element.14.wu_ref, ...), custom_call_target="tpu_custom_call" | custom-call | tf_op jit(solution)/shard_map/pallas_call | solution.py:346
  59.0 0.1 collective-permute-start.1
  59.2 0.0 copy-done
  59.2 0.0 copy-done.1
  59.2 1.1 %shard_map.134 = (f32[192,1792]{1,0:T(8,128)S(1)}, bf16[6,128,512]{2,1,0:T(8,128)(2,1)S(1)}) custom-call(bf16[192,512]{1,0:T(8,128)(2,1)S(1)} %get-tuple-element.17.hidden_ref, bf16[512,1792]{1,0:T(8,128)(2,1)S(1)} %get-tuple-element.18.wd_ref, s32[1]{0:T(128)S(6)} %copy.14.len_ref, s32[8,16]{1,0:T(8,128)S(1)} %bitcast.13, s32[8,16]{1,0:T(8,128)S(1)} %bitcast.14), custom_call_target="tpu_custom_call" | custom-call | tf_op jit(solution)/shard_map/pallas_call | solution.py:356
  60.3 0.3 collective-permute-done.1.hidden_ref
  60.6 0.0 collective-permute-done.2.wd_ref
  60.6 1.0 %shard_map.135 = bf16[512,768]{1,0:T(8,128)(2,1)S(1)} custom-call(f32[192,1792]{1,0:T(8,128)S(1)} %get-tuple-element.20.sum_ref, bf16[192,512]{1,0:T(8,128)(2,1)S(1)} %collective-permute-done.1.hidden_ref, bf16[1,512,3584]{2,1,0:T(8,128)(2,1)S(1)} %collective-permute-done.2.wd_ref, bf16[16,512]{1,0:T(8,128)(2,1)S(1)} %get-tuple-element.21.attn_ref), custom_call_target="tpu_custom_call" | custom-call | tf_op jit(solution)/shard_map/pallas_call | solution.py:364
  61.6 28.8 %all_to_all.11 = bf16[64,8,768]{2,1,0:T(8,128)(2,1)S(1)} all-to-all(bf16[64,8,768]{2,1,0:T(8,128)(2,1)S(1)} %bitcast.9), channel_id=1, replica_groups=mesh['groups'=2,'expert'=64,'tensor'=2] {'expert'}, dimensions={0} | all-to-all | bytes 1572864 | tf_op jit(solution)/shard_map/all_to_all | solution.py:318
  90.4 1.1 %shard_map.136 = (bf16[16,1792]{1,0:T(8,128)(2,1)S(1)}, bf16[64,512]{1,0:T(8,128)(2,1)}) custom-call(bf16[6,128,512]{2,1,0:T(8,128)(2,1)S(1)} %get-tuple-element.19.weigh_ref, bf16[512,768]{1,0:T(8,128)(2,1)S(1)} %bitcast.7), custom_call_target="tpu_custom_call" | custom-call | tf_op jit(solution)/shard_map/pallas_call | solution.py:371
  91.4 2.5 %collective-permute-start.3 = (bf16[16,1792]{1,0:T(8,128)(2,1)S(1)}, bf16[16,1792]{1,0:T(8,128)(2,1)S(1)}, u32[]{:S(2)}, u32[]{:S(2)}) collective-permute-start(bf16[16,1792]{1,0:T(8,128)(2,1)S(1)} %get-tuple-element.22), channel_id=1, source_target_pairs={{0,1},{1,0},{2,3},{3,2},{4,5},{5,4},{6,7},{7,6},{8,9},{9,8},{10,11... | collective-permute-start | bytes 172040 | tf_op jit(solution)/shard_map/ppermute | solution.py:379
  94.0 0.9 collective-permute-done.3
  94.9 0.7 maximum_select_fusion
Async XLA Ops:
  0.6 59.9 %collective-permute-start.2 = (bf16[1,512,3584]{2,1,0:T(8,128)(2,1)}, bf16[1,512,3584]{2,1,0:T(8,128)(2,1)S(1)}, u32[]{:S(2)}, u32[]{:S(2)}) collective-permute-start(bf16[1,512,3584]{2,1,0:T(8,128)(2,1)} %wd_hbm.1), channel_id=1, source_target_pairs={{0,1},{1,0},{2,3},{3,2},{4,5},{5,4},{6,7},{7,6},{8,9},{9,8},{10,11... | collective-permute-start | bytes 11010056 | tf_op jit(solution)/shard_map/ppermute | solution.py:332
  52.0 5.4 %collective-permute-start = (bf16[512,768]{1,0:T(8,128)(2,1)S(1)}, bf16[512,768]{1,0:T(8,128)(2,1)S(1)}, u32[]{:S(2)}, u32[]{:S(2)}) collective-permute-start(bf16[512,768]{1,0:T(8,128)(2,1)S(1)} %bitcast.10), channel_id=1, source_target_pairs={{0,1},{1,0},{2,3},{3,2},{4,5},{5,4},{6,7},{7,6},{8,9},{9,8},{10,11... | collective-permute-start | bytes 2359304 | tf_op jit(solution)/shard_map/ppermute | solution.py:331
  57.5 1.7 %copy-start = (s32[16,8]{0,1:T(8,128)S(1)}, s32[16,8]{0,1:T(8,128)}, u32[]{:S(2)}) copy-start(s32[16,8]{0,1:T(8,128)} %param.14) | copy-start | bytes 1540
  57.5 1.7 %copy-start.1 = (s32[16,8]{0,1:T(8,128)S(1)}, s32[16,8]{0,1:T(8,128)}, u32[]{:S(2)}) copy-start(s32[16,8]{0,1:T(8,128)} %param.15) | copy-start | bytes 1540
  59.0 1.6 %collective-permute-start.1 = (bf16[192,512]{1,0:T(8,128)(2,1)S(1)}, bf16[192,512]{1,0:T(8,128)(2,1)S(1)}, u32[]{:S(2)}, u32[]{:S(2)}) collective-permute-start(bf16[192,512]{1,0:T(8,128)(2,1)S(1)} %get-tuple-element.17.hidden_ref), channel_id=1, source_target_pairs={{0,1},{1,0},{2,3},{3,2},{4,5},{5,4},{6,7},{7,6},{8,9},{9,8},{10,11... | collective-permute-start | bytes 589832 | tf_op jit(solution)/shard_map/ppermute | solution.py:355
  91.4 3.4 %collective-permute-start.3 = (bf16[16,1792]{1,0:T(8,128)(2,1)S(1)}, bf16[16,1792]{1,0:T(8,128)(2,1)S(1)}, u32[]{:S(2)}, u32[]{:S(2)}) collective-permute-start(bf16[16,1792]{1,0:T(8,128)(2,1)S(1)} %get-tuple-element.22), channel_id=1, source_target_pairs={{0,1},{1,0},{2,3},{3,2},{4,5},{5,4},{6,7},{7,6},{8,9},{9,8},{10,11... | collective-permute-start | bytes 172040 | tf_op jit(solution)/shard_map/ppermute | solution.py:379

commit v4 on v3

--- a/solution.py
+++ b/solution.py
@@ -52,32 +52,36 @@
 
 
 def pack_kernel(
-    len_ref, ctx_hbm, hid_hbm, ids_hbm, ql_hbm, qr_hbm, kl_hbm, kr_hbm,
-    out_ref,
+    len_ref, ctx_hbm, hid_hbm, ids_hbm, ql_hbm, qr_hbm, kl_hbm, kr_hbm, wg_hbm, wd_hbm,
+    out_ref, first_gate_ref, give_ref,
     ctx_ref, hid_ref, ids_ref, ql_ref, qr_ref, kl_ref, kr_ref, sems,
 ):
-    pairs = (
-        (ql_hbm, ql_ref), (kl_hbm, kl_ref), (qr_hbm, qr_ref), (kr_hbm, kr_ref), (ctx_hbm, ctx_ref),
-        (ids_hbm, ids_ref), (hid_hbm, hid_ref),
-    )
-    copies = copied(pairs, sems)
     expert, tensor = lax.axis_index("expert"), lax.axis_index("tensor")
+    half = hid_ref.shape[1] // 2
+    mine = pl.ds(pl.multiple_of(tensor * half, half), half)
+    theirs = pl.ds(pl.multiple_of((1 - tensor) * half, half), half)
+    copies = copied(
+        (
+            (ql_hbm, ql_ref), (kl_hbm, kl_ref), (qr_hbm, qr_ref), (kr_hbm, kr_ref),
+            (ctx_hbm, ctx_ref), (ids_hbm, ids_ref), (hid_hbm, hid_ref),
+            (wd_hbm.at[0, :, theirs], give_ref), (wg_hbm.at[0, mine, :], first_gate_ref),
+        ),
+        sems,
+    )
     total_rows, width = out_ref.shape
     owners = total_rows // SUB
     piece = width // CAP
     tok = hid_ref.shape[0]
-    half = hid_ref.shape[1] // 2
     batch, heads, lat = ql_ref.shape
     ctx_dev = kl_ref.shape[1]
 
     block = SUB * tok
-    row, col = iota((total_rows, block), 0), iota((total_rows, block), 1)
-    kept = (row % SUB == col // tok) & (col < block - tok)
-    spread = ones_where(iota((total_rows, owners), 0) // SUB == iota((total_rows, owners), 1))
+    sub, lane = iota((SUB, block), 0), iota((SUB, block), 1)
+    kept = (sub == lane // tok) & (lane < block - tok)
     last = ones_where(
         iota((total_rows, owners), 0) == iota((total_rows, owners), 1) * SUB + (SUB - 1)
     )
-    for copy in copies[:5]:
+    for copy in copies[:7]:
         copy.wait()
     parts = []
     for b in range(batch):
@@ -96,8 +100,6 @@
         parts.append(jnp.concatenate([mean, stats], axis=1).astype(bf16))
     attn = jnp.concatenate(parts, axis=0)
 
-    for copy in copies[5:]:
-        copy.wait()
     _, _, match, rank = routing(ids_ref[...], owners, tok, len_ref[0])
     hidden = hid_ref[...]
     source = jnp.where(tensor == 0, hidden[:, :half], hidden[:, half:])
@@ -105,10 +107,14 @@
     stacked.append(jnp.zeros((tok, piece), bf16))
     stacked = jnp.concatenate(stacked, axis=0)
     for c in range(CAP):
-        mine = jnp.where(rank == c, match, 0.0).astype(bf16)
-        lhs = jnp.where(kept, dot(spread, mine), 0.0).astype(bf16)
+        mine = jnp.where(rank == c, match, 0.0)
+        lhs = jnp.where(kept, mine[:, None, :], 0.0).reshape(total_rows, block).astype(bf16)
         at = slice(c * piece, (c + 1) * piece)
-        out_ref[:, at] = (dot(lhs, stacked) + dot(last, attn[:, at])).astype(bf16)
+        lhs = jnp.concatenate([lhs, last], axis=1)
+        rhs = jnp.concatenate([stacked, attn[:, at]], axis=0)
+        out_ref[:, at] = dot(lhs, rhs).astype(bf16)
+    for copy in copies[7:]:
+        copy.wait()
 
 
 def sort_rows(arrived, rows):
@@ -140,9 +146,9 @@
 
 
 def own_kernel(
-    own_ref, wg_hbm, wu_hbm,
+    own_ref, wg_ref, wg_hbm, wu_hbm,
     gate_ref, upper_ref, attn_ref, next_gate_ref, next_up_ref,
-    wg, wu, rows, sems,
+    wu, rows, sems,
 ):
     half = rows.shape[1]
     lat = attn_ref.shape[1]
@@ -151,7 +157,6 @@
     theirs = pl.ds(pl.multiple_of((1 - tensor) * half, half), half)
     copies = copied(
         (
-            (wg_hbm.at[0, mine, :], wg),
             (wu_hbm.at[0, mine, :], wu),
             (wg_hbm.at[0, theirs, :], next_gate_ref),
             (wu_hbm.at[0, theirs, :], next_up_ref),
@@ -166,12 +171,11 @@
     weighted = jnp.sum(share * arrived[:, :lat], axis=0, keepdims=True)
     done = weighted / jnp.sum(share, axis=0, keepdims=True)
     attn_ref[...] = jnp.broadcast_to(done, attn_ref.shape).astype(bf16)
+    gate_ref[...] = dot(rows[...], wg_ref[...])
     copies[0].wait()
-    gate_ref[...] = dot(rows[...], wg[...])
+    upper_ref[...] = dot(rows[...], wu[...])
     copies[1].wait()
-    upper_ref[...] = dot(rows[...], wu[...])
     copies[2].wait()
-    copies[3].wait()
 
 
 def other_kernel(
@@ -199,8 +203,7 @@
     owners = total_rows // SUB
     piece = width // CAP
     lat = attn_ref.shape[1]
-    mine = pl.ds(pl.multiple_of(lax.axis_index("tensor") * sum_ref.shape[1], sum_ref.shape[1]), sum_ref.shape[1])
-    whole = (sum_ref[...] + dot(hidden_ref[...], wd_ref[0, :, mine])).astype(bf16)
+    whole = (sum_ref[...] + dot(hidden_ref[...], wd_ref[...])).astype(bf16)
     part = owners // BLOCKS
     size = SUB * part
     row, col = iota((size, size), 0), iota((size, size), 1)
@@ -319,35 +322,31 @@
 
     ids_t, gate_t = expert_ids.T, gate_num.T
     arrays = (hidden_in, ids_t, q_latent, q_rope, kv_latent, kv_rope)
-    packed = call(
+    half_weights = pltpu.VMEM((half, hidden_units), bf16)
+    half_down = pltpu.VMEM((hidden_units, half), bf16)
+    packed, first_gate, given = call(
         pack_kernel,
-        pltpu.VMEM((total_rows, width), bf16),
-        [smem()] + [hbm() for _ in range(7)],
+        (pltpu.VMEM((total_rows, width), bf16), half_weights, half_down),
+        [smem()] + [hbm() for _ in range(9)],
         [pltpu.SMEM(ctx_len.shape, ctx_len.dtype)]
         + [pltpu.VMEM(a.shape, a.dtype) for a in arrays]
-        + [pltpu.SemaphoreType.DMA((7,))],
-    )(batch_len, *in_hbm(ctx_len, *arrays))
+        + [pltpu.SemaphoreType.DMA((9,))],
+    )(batch_len, *in_hbm(ctx_len, *arrays, w_gate, w_down))
     own = exchanged(packed)
     other = lax.ppermute(own, "tensor", swap)
-    down_other = lax.ppermute(w_down, "tensor", swap)
+    down_other = lax.ppermute(given, "tensor", swap)
     partial = jax.ShapeDtypeStruct((slots, hidden_units), f32)
-    half_weights = pltpu.VMEM((half, hidden_units), bf16)
     gate, upper, attn, next_gate, next_up = call(
         own_kernel,
         (partial, partial, jax.ShapeDtypeStruct((16, lat), bf16), half_weights, half_weights),
-        [vmem(), hbm(), hbm()],
-        [
-            half_weights,
-            half_weights,
-            pltpu.VMEM((slots, half), bf16),
-            pltpu.SemaphoreType.DMA((4,)),
-        ],
-    )(own, *in_hbm(w_gate, w_up))
+        [vmem(), vmem(), hbm(), hbm()],
+        [half_weights, pltpu.VMEM((slots, half), bf16), pltpu.SemaphoreType.DMA((3,))],
+    )(own, *in_vmem(first_gate), *in_hbm(w_gate, w_up))
     hidden, next_down = call(
         other_kernel,
         (
             jax.ShapeDtypeStruct((slots, hidden_units), bf16),
-            pltpu.VMEM((hidden_units, half), bf16),
+            half_down,
         ),
         [vmem() for _ in range(5)] + [hbm()],
         [pltpu.VMEM((slots, half), bf16), pltpu.SemaphoreType.DMA((1,))],
@@ -372,7 +371,7 @@
         sum_kernel,
         (
             jax.ShapeDtypeStruct((tok, half), bf16),
-            jax.ShapeDtypeStruct((batch * heads, lat), bf16),
+            pltpu.VMEM((batch * heads, lat), bf16),
         ),
         [vmem(), vmem()],
     )(weights, back)

time: 95.8 us -> 93.7 us (0.978)
  blocking collectives: 56.3 us -> 27.9 us
  starting transfers between devices: 25.1 us -> 37.3 us
  waiting for transfers between devices: 1.19 us -> 12.2 us
  local copies, waits for them, and re-layouts: 0.01 us -> 1.9 us
  Pallas kernels: 10.9 us -> 12 us
    all_to_all x2 -> x1, blocking collectives: 56.3 us -> 27.9 us  [exchanged(): lax.all_to_all(whole, 'expert', 0, 0, tiled=True).reshape(total_rows, width)]
    all_to_all x0 -> x1, starting transfers between devices: none -> 21.8 us  [exchanged(): lax.all_to_all(whole, 'expert', 0, 0, tiled=True).reshape(total_rows, width)]
    ppermute x1, starting transfers between devices: 20.5 us -> 5.24 us  [local(): down_other = lax.ppermute(given, 'tensor', swap)]
    all_to_all x0 -> x1, waiting for transfers between devices: none -> 11.7 us  [exchanged(): lax.all_to_all(whole, 'expert', 0, 0, tiled=True).reshape(total_rows, width)]
    ppermute x1, starting transfers between devices: 1.85 us -> 7.43 us  [local(): other = lax.ppermute(own, 'tensor', swap)]
    unnamed x4 -> x7, local copies, waits for them, and re-layouts: 0.01 us -> 1.9 us
    pallas_call x1, Pallas kernels: 0.97 us -> 2.42 us  [local(): call(back_kernel, jax.ShapeDtypeStruct((total_rows, width), bf16), [vmem(...]
  transfers between devices with their start and end apart: 4 -> 5, of which waited for: 2 -> 3; matrix products, arithmetic and copies ran while one was open for 0% -> 1% of each run, Pallas kernels for 9% -> 6%
where the time goes in v4:
time: 93.7 us; the launch traced here: 93.4 us
  starting transfers between devices  37.3 us (40%)
  blocking collectives  27.9 us (30%)
  waiting for transfers between devices  12.2 us (13%)
  Pallas kernels  12 us (13%)
  local copies, waits for them, and re-layouts  1.9 us (2%)
  between operations  1.4 us (1%)
    all_to_all x1, blocking collectives, exchanged(): lax.all_to_all(whole, 'expert', 0, 0, tiled=True).reshape(total_rows, width)  27.9 us
    all_to_all x1, starting transfers between devices, exchanged(): lax.all_to_all(whole, 'expert', 0, 0, tiled=True).reshape(total_rows, width)  21.8 us
    all_to_all x1, waiting for transfers between devices, exchanged(): lax.all_to_all(whole, 'expert', 0, 0, tiled=True).reshape(total_rows, width)  11.7 us
    ppermute x1, starting transfers between devices, local(): other = lax.ppermute(own, 'tensor', swap)  7.43 us
    ppermute x1, starting transfers between devices, local(): down_other = lax.ppermute(given, 'tensor', swap)  5.24 us
    pallas_call x1, Pallas kernels, local(): call(own_kernel, (partial, partial, jax.ShapeDtypeStruct((16, lat), bf16)...  3.27 us
    pallas_call x1, Pallas kernels, local(): call(pack_kernel, (pltpu.VMEM((total_rows, width), bf16), half_weights, h...  3.24 us
    ppermute x1, starting transfers between devices, local(): moe_other = lax.ppermute(moe_half, 'tensor', swap)  2.67 us
  transfers between devices with their start and end apart: 5, of which 3 were waited for; matrix products, arithmetic and copies ran while one was open for 1% of the time, Pallas kernels for 6%

profile of v4, /device:TPU:513, one launch (start us, length us, event | category | flops | bytes accessed | tf_op | source)
XLA Modules:
  0.0 93.4 jit_solution(16373229941433234646)
XLA Ops:
  1.3 3.2 %shard_map.131 = (bf16[512,768]{1,0:T(8,128)(2,1)}, bf16[1792,512]{1,0:T(8,128)(2,1)S(1)}, bf16[512,1792]{1,0:T(8,128)(2,1)S(1)}) custom-call(s32[1]{0:T(128)S(6)} %copy.15.len_ref, s32[2]{0:T(128)} %ctx_hbm.1, bf16[16,3584]{1,0:T(8,128)(2,1)} %hid_hbm.1, s32[8,16]{1,0:T(8,128)} %bitcast.12, bf16[2,32,512]{2,1,0:T(8,128)(2,1)} %ql_hbm.1, ...), custom_call_target="tpu_custom_call" | custom-call | tf_op jit(solution)/shard_map/pallas_call | solution.py:327
  4.5 0.0 copy-start.2
  4.5 1.3 %copy-done.2 = bf16[512,1792]{1,0:T(8,128)(2,1)} copy-done((bf16[512,1792]{1,0:T(8,128)(2,1)}, bf16[512,1792]{1,0:T(8,128)(2,1)S(1)}, u32[]{:S(2)}) %copy-start.2) | copy-done | bytes 1835032
  5.8 21.8 %all-to-all-start = ((bf16[64,8,768]{2,1,0:T(8,128)(2,1)}), bf16[64,8,768]{2,1,0:T(8,128)(2,1)S(1)}, u32[]{:S(2)}, u32[]{:S(2)}) async-start(bf16[64,8,768]{2,1,0:T(8,128)(2,1)} %bitcast.1), calls=%async_computation | async-start | bytes 1572864 | tf_op jit(solution)/shard_map/all_to_all | solution.py:321
  27.6 5.2 %collective-permute-start.2 = (bf16[512,1792]{1,0:T(8,128)(2,1)}, bf16[512,1792]{1,0:T(8,128)(2,1)}, u32[]{:S(2)}, u32[]{:S(2)}) collective-permute-start(bf16[512,1792]{1,0:T(8,128)(2,1)} %copy-done.2), channel_id=1, source_target_pairs={{0,1},{1,0},{2,3},{3,2},{4,5},{5,4},{6,7},{7,6},{8,9},{9,8},{10,11... | collective-permute-start | bytes 5505032 | tf_op jit(solution)/shard_map/ppermute | solution.py:337
  32.8 11.7 %all-to-all-done = bf16[64,8,768]{2,1,0:T(8,128)(2,1)S(1)} async-done(((bf16[64,8,768]{2,1,0:T(8,128)(2,1)}), bf16[64,8,768]{2,1,0:T(8,128)(2,1)S(1)}, u32[]{:S(2)}, u32[]{:S(2)}) %all-to-all-start) | async-done | bytes 786464 | tf_op jit(solution)/shard_map/all_to_all | solution.py:321
  44.5 7.4 %collective-permute-start = (bf16[512,768]{1,0:T(8,128)(2,1)S(1)}, bf16[512,768]{1,0:T(8,128)(2,1)S(1)}, u32[]{:S(2)}, u32[]{:S(2)}) collective-permute-start(bf16[512,768]{1,0:T(8,128)(2,1)S(1)} %bitcast.8), channel_id=1, source_target_pairs={{0,1},{1,0},{2,3},{3,2},{4,5},{5,4},{6,7},{7,6},{8,9},{9,8},{10,11... | collective-permute-start | bytes 2359304 | tf_op jit(solution)/shard_map/ppermute | solution.py:336
  52.0 3.3 %shard_map.132 = (f32[192,512]{1,0:T(8,128)S(1)}, f32[192,512]{1,0:T(8,128)S(1)}, bf16[16,512]{1,0:T(8,128)(2,1)S(1)}, bf16[1792,512]{1,0:T(8,128)(2,1)S(1)}, bf16[1792,512]{1,0:T(8,128)(2,1)S(1)}) custom-call(bf16[512,768]{1,0:T(8,128)(2,1)S(1)} %bitcast.9, bf16[1792,512]{1,0:T(8,128)(2,1)S(1)} %get-tuple-element.17.wg_ref, bf16[1,3584,512]{2,1,0:T(8,128)(2,1)} %wg_hbm.3, ...), custom_call_target="tpu_custom_call" | custom-call | tf_op jit(solution)/shard_map/pallas_call | solution.py:339
  55.2 0.0 collective-permute-done.other_ref
  55.3 0.0 copy-start
  55.3 0.0 copy-start.1
  55.3 1.5 %shard_map.133 = (bf16[192,512]{1,0:T(8,128)(2,1)S(1)}, bf16[512,1792]{1,0:T(8,128)(2,1)S(1)}) custom-call(bf16[512,768]{1,0:T(8,128)(2,1)S(1)} %collective-permute-done.other_ref, bf16[1792,512]{1,0:T(8,128)(2,1)S(1)} %get-tuple-element.18.wg_ref, bf16[1792,512]{1,0:T(8,128)(2,1)S(1)} %get-tuple-element.19.wu_ref, ...), custom_call_target="tpu_custom_call" | custom-call | tf_op jit(solution)/shard_map/pallas_call | solution.py:345
  56.8 0.1 collective-permute-start.1
  57.0 0.0 copy-done
  57.0 0.0 copy-done.1
  57.0 1.1 %shard_map.134 = (f32[192,1792]{1,0:T(8,128)S(1)}, bf16[6,128,512]{2,1,0:T(8,128)(2,1)S(1)}) custom-call(bf16[192,512]{1,0:T(8,128)(2,1)S(1)} %get-tuple-element.22.hidden_ref, bf16[512,1792]{1,0:T(8,128)(2,1)S(1)} %get-tuple-element.23.wd_ref, s32[1]{0:T(128)S(6)} %copy.15.len_ref, s32[8,16]{1,0:T(8,128)S(1)} %bitcast.13, s32[8,16]{1,0:T(8,128)S(1)} %bitcast.14), custom_call_target="tpu_custom_call" | custom-call | tf_op jit(solution)/shard_map/pallas_call | solution.py:355
  58.1 0.0 collective-permute-done.2.wd_ref
  58.1 0.3 collective-permute-done.1.hidden_ref
  58.4 2.4 %shard_map.135 = bf16[512,768]{1,0:T(8,128)(2,1)S(1)} custom-call(f32[192,1792]{1,0:T(8,128)S(1)} %get-tuple-element.25.sum_ref, bf16[192,512]{1,0:T(8,128)(2,1)S(1)} %collective-permute-done.1.hidden_ref, bf16[512,1792]{1,0:T(8,128)(2,1)} %collective-permute-done.2.wd_ref, bf16[16,512]{1,0:T(8,128)(2,1)S(1)} %get-tuple-element.27.attn_ref), custom_call_target="tpu_custom_call" | custom-call | tf_op jit(solution)/shard_map/pallas_call | solution.py:363
  60.8 27.9 %all_to_all.10 = bf16[64,8,768]{2,1,0:T(8,128)(2,1)S(1)} all-to-all(bf16[64,8,768]{2,1,0:T(8,128)(2,1)S(1)} %bitcast.10), channel_id=1, replica_groups=mesh['groups'=2,'expert'=64,'tensor'=2] {'expert'}, dimensions={0} | all-to-all | bytes 1572864 | tf_op jit(solution)/shard_map/all_to_all | solution.py:321
  88.7 0.5 shard_map.136
  89.2 2.7 %collective-permute-start.3 = (bf16[16,1792]{1,0:T(8,128)(2,1)S(1)}, bf16[16,1792]{1,0:T(8,128)(2,1)S(1)}, u32[]{:S(2)}, u32[]{:S(2)}) collective-permute-start(bf16[16,1792]{1,0:T(8,128)(2,1)S(1)} %get-tuple-element.28), channel_id=1, source_target_pairs={{0,1},{1,0},{2,3},{3,2},{4,5},{5,4},{6,7},{7,6},{8,9},{9,8},{10,11... | collective-permute-start | bytes 172040 | tf_op jit(solution)/shard_map/ppermute | solution.py:378
  91.8 0.6 copy.14
  92.5 0.3 collective-permute-done.3
  92.7 0.7 maximum_select_fusion
Async XLA Ops:
  4.5 1.3 %copy-start.2 = (bf16[512,1792]{1,0:T(8,128)(2,1)}, bf16[512,1792]{1,0:T(8,128)(2,1)S(1)}, u32[]{:S(2)}) copy-start(bf16[512,1792]{1,0:T(8,128)(2,1)S(1)} %get-tuple-element.26) | copy-start | bytes 5505028
  5.8 38.7 %all-to-all-start = ((bf16[64,8,768]{2,1,0:T(8,128)(2,1)}), bf16[64,8,768]{2,1,0:T(8,128)(2,1)S(1)}, u32[]{:S(2)}, u32[]{:S(2)}) async-start(bf16[64,8,768]{2,1,0:T(8,128)(2,1)} %bitcast.1), calls=%async_computation | async-start | bytes 1572864 | tf_op jit(solution)/shard_map/all_to_all | solution.py:321
  27.6 30.5 %collective-permute-start.2 = (bf16[512,1792]{1,0:T(8,128)(2,1)}, bf16[512,1792]{1,0:T(8,128)(2,1)}, u32[]{:S(2)}, u32[]{:S(2)}) collective-permute-start(bf16[512,1792]{1,0:T(8,128)(2,1)} %copy-done.2), channel_id=1, source_target_pairs={{0,1},{1,0},{2,3},{3,2},{4,5},{5,4},{6,7},{7,6},{8,9},{9,8},{10,11... | collective-permute-start | bytes 5505032 | tf_op jit(solution)/shard_map/ppermute | solution.py:337
  44.5 10.7 %collective-permute-start = (bf16[512,768]{1,0:T(8,128)(2,1)S(1)}, bf16[512,768]{1,0:T(8,128)(2,1)S(1)}, u32[]{:S(2)}, u32[]{:S(2)}) collective-permute-start(bf16[512,768]{1,0:T(8,128)(2,1)S(1)} %bitcast.8), channel_id=1, source_target_pairs={{0,1},{1,0},{2,3},{3,2},{4,5},{5,4},{6,7},{7,6},{8,9},{9,8},{10,11... | collective-permute-start | bytes 2359304 | tf_op jit(solution)/shard_map/ppermute | solution.py:336
  55.3 1.7 %copy-start = (s32[16,8]{0,1:T(8,128)S(1)}, s32[16,8]{0,1:T(8,128)}, u32[]{:S(2)}) copy-start(s32[16,8]{0,1:T(8,128)} %param.14) | copy-start | bytes 1540
  55.3 1.7 %copy-start.1 = (s32[16,8]{0,1:T(8,128)S(1)}, s32[16,8]{0,1:T(8,128)}, u32[]{:S(2)}) copy-start(s32[16,8]{0,1:T(8,128)} %param.15) | copy-start | bytes 1540
  56.8 1.6 %collective-permute-start.1 = (bf16[192,512]{1,0:T(8,128)(2,1)S(1)}, bf16[192,512]{1,0:T(8,128)(2,1)S(1)}, u32[]{:S(2)}, u32[]{:S(2)}) collective-permute-start(bf16[192,512]{1,0:T(8,128)(2,1)S(1)} %get-tuple-element.22.hidden_ref), channel_id=1, source_target_pairs={{0,1},{1,0},{2,3},{3,2},{4,5},{5,4},{6,7},{7,6},{8,9},{9,8},{10,11... | collective-permute-start | bytes 589832 | tf_op jit(solution)/shard_map/ppermute | solution.py:354
  89.2 3.6 %collective-permute-start.3 = (bf16[16,1792]{1,0:T(8,128)(2,1)S(1)}, bf16[16,1792]{1,0:T(8,128)(2,1)S(1)}, u32[]{:S(2)}, u32[]{:S(2)}) collective-permute-start(bf16[16,1792]{1,0:T(8,128)(2,1)S(1)} %get-tuple-element.28), channel_id=1, source_target_pairs={{0,1},{1,0},{2,3},{3,2},{4,5},{5,4},{6,7},{7,6},{8,9},{9,8},{10,11... | collective-permute-start | bytes 172040 | tf_op jit(solution)/shard_map/ppermute | solution.py:378

commit v5 on v4

--- a/solution.py
+++ b/solution.py
@@ -52,8 +52,8 @@
 
 
 def pack_kernel(
-    len_ref, ctx_hbm, hid_hbm, ids_hbm, ql_hbm, qr_hbm, kl_hbm, kr_hbm, wg_hbm, wd_hbm,
-    out_ref, first_gate_ref, give_ref,
+    len_ref, ctx_hbm, hid_hbm, ids_hbm, ql_hbm, qr_hbm, kl_hbm, kr_hbm, wd_hbm,
+    out_ref, give_ref,
     ctx_ref, hid_ref, ids_ref, ql_ref, qr_ref, kl_ref, kr_ref, sems,
 ):
     expert, tensor = lax.axis_index("expert"), lax.axis_index("tensor")
@@ -64,7 +64,7 @@
         (
             (ql_hbm, ql_ref), (kl_hbm, kl_ref), (qr_hbm, qr_ref), (kr_hbm, kr_ref),
             (ctx_hbm, ctx_ref), (ids_hbm, ids_ref), (hid_hbm, hid_ref),
-            (wd_hbm.at[0, :, theirs], give_ref), (wg_hbm.at[0, mine, :], first_gate_ref),
+            (wd_hbm.at[0, :, theirs], give_ref),
         ),
         sems,
     )
@@ -146,8 +146,8 @@
 
 
 def own_kernel(
-    own_ref, wg_ref, wg_hbm, wu_hbm,
-    gate_ref, upper_ref, attn_ref, next_gate_ref, next_up_ref,
+    own_ref, wg_ref, wu_hbm,
+    gate_ref, upper_ref, attn_ref, next_up_ref,
     wu, rows, sems,
 ):
     half = rows.shape[1]
@@ -155,14 +155,7 @@
     tensor = lax.axis_index("tensor")
     mine = pl.ds(pl.multiple_of(tensor * half, half), half)
     theirs = pl.ds(pl.multiple_of((1 - tensor) * half, half), half)
-    copies = copied(
-        (
-            (wu_hbm.at[0, mine, :], wu),
-            (wg_hbm.at[0, theirs, :], next_gate_ref),
-            (wu_hbm.at[0, theirs, :], next_up_ref),
-        ),
-        sems,
-    )
+    copies = copied(((wu_hbm.at[0, mine, :], wu), (wu_hbm.at[0, theirs, :], next_up_ref)), sems)
     arrived = sort_rows(own_ref[...], rows)
     stats = [arrived[:, lat + k : lat + k + 1] for k in range(6)]
     top = stats[0] + stats[1] + stats[2]
@@ -171,31 +164,29 @@
     weighted = jnp.sum(share * arrived[:, :lat], axis=0, keepdims=True)
     done = weighted / jnp.sum(share, axis=0, keepdims=True)
     attn_ref[...] = jnp.broadcast_to(done, attn_ref.shape).astype(bf16)
-    gate_ref[...] = dot(rows[...], wg_ref[...])
+    gate_ref[...] = dot(rows[...], wg_ref[0, mine, :])
     copies[0].wait()
     upper_ref[...] = dot(rows[...], wu[...])
     copies[1].wait()
-    copies[2].wait()
-
-
-def other_kernel(
-    other_ref, wg_ref, wu_ref, gate_ref, upper_ref, wd_hbm,
-    hidden_ref, next_down_ref,
-    rows, sems,
-):
+
+
+def other_kernel(other_ref, wg_ref, wu_ref, gate_ref, upper_ref, hidden_ref, rows):
     half = rows.shape[1]
-    mine = pl.ds(pl.multiple_of(lax.axis_index("tensor") * half, half), half)
-    copies = copied(((wd_hbm.at[0, :, mine], next_down_ref),), sems)
+    theirs = pl.ds(pl.multiple_of((1 - lax.axis_index("tensor")) * half, half), half)
     sort_rows(other_ref[...], rows)
-    gate = gate_ref[...] + dot(rows[...], wg_ref[...])
+    gate = gate_ref[...] + dot(rows[...], wg_ref[0, theirs, :])
     upper = upper_ref[...] + dot(rows[...], wu_ref[...])
     hidden_ref[...] = (gate / (1.0 + jnp.exp(-gate)) * upper).astype(bf16)
-    copies[0].wait()
-
-
-def down_kernel(hidden_ref, wd_ref, len_ref, ids_ref, gate_ref, sum_ref, weigh_ref):
-    sum_ref[...] = dot(hidden_ref[...], wd_ref[...])
+
+
+def weigh_kernel(hidden_ref, len_ref, ids_ref, gate_ref, weigh_ref):
     weigh(len_ref, ids_ref, gate_ref, weigh_ref)
+
+
+def down_kernel(hidden_ref, wd_ref, weigh_ref, sum_ref):
+    half = sum_ref.shape[1]
+    mine = pl.ds(pl.multiple_of(lax.axis_index("tensor") * half, half), half)
+    sum_ref[...] = dot(hidden_ref[...], wd_ref[0, :, mine])
 
 
 def back_kernel(sum_ref, hidden_ref, wd_ref, attn_ref, out_ref, rows):
@@ -322,44 +313,43 @@
 
     ids_t, gate_t = expert_ids.T, gate_num.T
     arrays = (hidden_in, ids_t, q_latent, q_rope, kv_latent, kv_rope)
-    half_weights = pltpu.VMEM((half, hidden_units), bf16)
     half_down = pltpu.VMEM((hidden_units, half), bf16)
-    packed, first_gate, given = call(
+    packed, given = call(
         pack_kernel,
-        (pltpu.VMEM((total_rows, width), bf16), half_weights, half_down),
-        [smem()] + [hbm() for _ in range(9)],
+        (pltpu.VMEM((total_rows, width), bf16), half_down),
+        [smem()] + [hbm() for _ in range(8)],
         [pltpu.SMEM(ctx_len.shape, ctx_len.dtype)]
         + [pltpu.VMEM(a.shape, a.dtype) for a in arrays]
-        + [pltpu.SemaphoreType.DMA((9,))],
-    )(batch_len, *in_hbm(ctx_len, *arrays, w_gate, w_down))
+        + [pltpu.SemaphoreType.DMA((8,))],
+    )(batch_len, *in_hbm(ctx_len, *arrays, w_down))
     own = exchanged(packed)
     other = lax.ppermute(own, "tensor", swap)
     down_other = lax.ppermute(given, "tensor", swap)
     partial = jax.ShapeDtypeStruct((slots, hidden_units), f32)
-    gate, upper, attn, next_gate, next_up = call(
+    half_up = pltpu.VMEM((half, hidden_units), bf16)
+    gate, upper, attn, next_up = call(
         own_kernel,
-        (partial, partial, jax.ShapeDtypeStruct((16, lat), bf16), half_weights, half_weights),
-        [vmem(), vmem(), hbm(), hbm()],
-        [half_weights, pltpu.VMEM((slots, half), bf16), pltpu.SemaphoreType.DMA((3,))],
-    )(own, *in_vmem(first_gate), *in_hbm(w_gate, w_up))
-    hidden, next_down = call(
+        (partial, partial, jax.ShapeDtypeStruct((16, lat), bf16), half_up),
+        [vmem(), vmem(), hbm()],
+        [half_up, pltpu.VMEM((slots, half), bf16), pltpu.SemaphoreType.DMA((2,))],
+    )(own, w_gate, *in_hbm(w_up))
+    hidden = call(
         other_kernel,
-        (
-            jax.ShapeDtypeStruct((slots, hidden_units), bf16),
-            half_down,
-        ),
-        [vmem() for _ in range(5)] + [hbm()],
-        [pltpu.VMEM((slots, half), bf16), pltpu.SemaphoreType.DMA((1,))],
-    )(other, *in_vmem(next_gate, next_up), gate, upper, *in_hbm(w_down))
+        jax.ShapeDtypeStruct((slots, hidden_units), bf16),
+        [vmem() for _ in range(5)],
+        [pltpu.VMEM((slots, half), bf16)],
+    )(other, w_gate, *in_vmem(next_up), gate, upper)
     hidden_other = lax.ppermute(hidden, "tensor", swap)
-    summed, weights = call(
+    weights = call(
+        weigh_kernel,
+        jax.ShapeDtypeStruct((2 * CAP, SUB * tok, total_rows), bf16),
+        [vmem(), smem(), vmem(), vmem()],
+    )(hidden, batch_len, ids_t, gate_t)
+    summed = call(
         down_kernel,
-        (
-            jax.ShapeDtypeStruct((slots, half), f32),
-            jax.ShapeDtypeStruct((2 * CAP, SUB * tok, total_rows), bf16),
-        ),
-        [vmem(), vmem(), smem(), vmem(), vmem()],
-    )(hidden, *in_vmem(next_down), batch_len, ids_t, gate_t)
+        jax.ShapeDtypeStruct((slots, half), f32),
+        [vmem(), vmem(), vmem()],
+    )(hidden, w_down, weights)
     returned = call(
         back_kernel,
         jax.ShapeDtypeStruct((total_rows, width), bf16),

time: 93.7 us -> 93.6 us (level)
  local copies, waits for them, and re-layouts: 1.9 us -> 4.13 us
  Pallas kernels: 12 us -> 9.89 us
    unnamed x7 -> x13, local copies, waits for them, and re-layouts: 1.9 us -> 4.13 us
    pallas_call x1, Pallas kernels: 2.42 us -> 0.92 us  [local(): call(back_kernel, jax.ShapeDtypeStruct((total_rows, width), bf16), [vmem(...]
    pallas_call x3 -> x4, Pallas kernels: 5.87 us -> 5.51 us  [the longest x1 3.16 us: local(): call(pack_kernel, (pltpu.VMEM((total_rows, width), bf16), half_down), [sm...]
where the time goes in v5:
time: 93.6 us; the launch traced here: 93.3 us
  starting transfers between devices  37.2 us (40%)
  blocking collectives  27.9 us (30%)
  waiting for transfers between devices  12.1 us (13%)
  Pallas kernels  9.89 us (11%)
  local copies, waits for them, and re-layouts  4.13 us (4%)
  between operations  1.39 us (1%)
    all_to_all x1, blocking collectives, exchanged(): lax.all_to_all(whole, 'expert', 0, 0, tiled=True).reshape(total_rows, width)  27.9 us
    all_to_all x1, starting transfers between devices, exchanged(): lax.all_to_all(whole, 'expert', 0, 0, tiled=True).reshape(total_rows, width)  21.8 us
    all_to_all x1, waiting for transfers between devices, exchanged(): lax.all_to_all(whole, 'expert', 0, 0, tiled=True).reshape(total_rows, width)  11.7 us
    ppermute x1, starting transfers between devices, local(): other = lax.ppermute(own, 'tensor', swap)  7.43 us
    ppermute x1, starting transfers between devices, local(): down_other = lax.ppermute(given, 'tensor', swap)  5.23 us
    unnamed x13, local copies, waits for them, and re-layouts  4.13 us
    pallas_call x1, Pallas kernels, local(): call(pack_kernel, (pltpu.VMEM((total_rows, width), bf16), half_down), [sm...  3.16 us
    pallas_call x1, Pallas kernels, local(): call(own_kernel, (partial, partial, jax.ShapeDtypeStruct((16, lat), bf16)...  3 us
  transfers between devices with their start and end apart: 5, of which 3 were waited for; matrix products, arithmetic and copies ran while one was open for 1% of the time, Pallas kernels for 6%

profile of v5, /device:TPU:513, one launch (start us, length us, event | category | flops | bytes accessed | tf_op | source)
XLA Modules:
  0.0 93.3 jit_solution(12138809558971308633)
XLA Ops:
  1.3 3.2 %shard_map.131 = (bf16[512,768]{1,0:T(8,128)(2,1)}, bf16[512,1792]{1,0:T(8,128)(2,1)S(1)}) custom-call(s32[1]{0:T(128)S(6)} %copy.15.len_ref, s32[2]{0:T(128)} %ctx_hbm.1, bf16[16,3584]{1,0:T(8,128)(2,1)} %hid_hbm.1, s32[8,16]{1,0:T(8,128)} %bitcast.12, bf16[2,32,512]{2,1,0:T(8,128)(2,1)} %ql_hbm.1, bf16[2,32,64]{2,1,0:T(8,128)(2,1)} %qr_hbm.1, ...), custom_call_target="tpu_custom_call" | custom-call | tf_op jit(solution)/shard_map/pallas_call | solution.py:317
  4.4 0.0 copy-start.5
  4.5 1.3 %copy-done.5 = bf16[512,1792]{1,0:T(8,128)(2,1)} copy-done((bf16[512,1792]{1,0:T(8,128)(2,1)}, bf16[512,1792]{1,0:T(8,128)(2,1)S(1)}, u32[]{:S(2)}) %copy-start.5) | copy-done | bytes 1835032
  5.7 21.8 %all-to-all-start = ((bf16[64,8,768]{2,1,0:T(8,128)(2,1)}), bf16[64,8,768]{2,1,0:T(8,128)(2,1)S(1)}, u32[]{:S(2)}, u32[]{:S(2)}) async-start(bf16[64,8,768]{2,1,0:T(8,128)(2,1)} %bitcast.1), calls=%async_computation | async-start | bytes 1572864 | tf_op jit(solution)/shard_map/all_to_all | solution.py:312
  27.5 5.2 %collective-permute-start.2 = (bf16[512,1792]{1,0:T(8,128)(2,1)}, bf16[512,1792]{1,0:T(8,128)(2,1)S(1)}, u32[]{:S(2)}, u32[]{:S(2)}) collective-permute-start(bf16[512,1792]{1,0:T(8,128)(2,1)} %copy-done.5), channel_id=1, source_target_pairs={{0,1},{1,0},{2,3},{3,2},{4,5},{5,4},{6,7},{7,6},{8,9},{9,8},{10,11... | collective-permute-start | bytes 5505032 | tf_op jit(solution)/shard_map/ppermute | solution.py:327
  32.8 11.7 %all-to-all-done = bf16[64,8,768]{2,1,0:T(8,128)(2,1)S(1)} async-done(((bf16[64,8,768]{2,1,0:T(8,128)(2,1)}), bf16[64,8,768]{2,1,0:T(8,128)(2,1)S(1)}, u32[]{:S(2)}, u32[]{:S(2)}) %all-to-all-start) | async-done | bytes 786464 | tf_op jit(solution)/shard_map/all_to_all | solution.py:312
  44.5 7.4 %collective-permute-start = (bf16[512,768]{1,0:T(8,128)(2,1)S(1)}, bf16[512,768]{1,0:T(8,128)(2,1)S(1)}, u32[]{:S(2)}, u32[]{:S(2)}) collective-permute-start(bf16[512,768]{1,0:T(8,128)(2,1)S(1)} %bitcast.10), channel_id=1, source_target_pairs={{0,1},{1,0},{2,3},{3,2},{4,5},{5,4},{6,7},{7,6},{8,9},{9,8},{10,11... | collective-permute-start | bytes 2359304 | tf_op jit(solution)/shard_map/ppermute | solution.py:326
  51.9 0.0 copy-start
  51.9 2.0 %copy-done = bf16[1,3584,512]{2,1,0:T(8,128)(2,1)S(1)} copy-done((bf16[1,3584,512]{2,1,0:T(8,128)(2,1)S(1)}, bf16[1,3584,512]{2,1,0:T(8,128)(2,1)}, u32[]{:S(2)}) %copy-start) | copy-done | bytes 3670040
  53.9 0.0 copy-start.1
  53.9 3.0 %shard_map.132 = (f32[192,512]{1,0:T(8,128)S(1)}, f32[192,512]{1,0:T(8,128)S(1)}, bf16[16,512]{1,0:T(8,128)(2,1)S(1)}, bf16[1792,512]{1,0:T(8,128)(2,1)S(1)}) custom-call(bf16[512,768]{1,0:T(8,128)(2,1)S(1)} %bitcast.11, bf16[1,3584,512]{2,1,0:T(8,128)(2,1)S(1)} %copy-done, bf16[1,3584,512]{2,1,0:T(8,128)(2,1)} %wu_hbm.1), custom_call_target="tpu_custom_call" | custom-call | tf_op jit(solution)/shard_map/pallas_call | solution.py:330
  56.9 0.0 collective-permute-done.other_ref
  57.0 0.1 copy-done.1
  57.1 0.0 copy-start.3
  57.1 0.0 copy-start.4
  57.1 0.0 copy-start.2
  57.1 1.1 %shard_map.133.hidden_ref = bf16[192,512]{1,0:T(8,128)(2,1)S(1)} custom-call(bf16[512,768]{1,0:T(8,128)(2,1)S(1)} %collective-permute-done.other_ref, bf16[1,3584,512]{2,1,0:T(8,128)(2,1)S(1)} %copy-done.1, bf16[1792,512]{1,0:T(8,128)(2,1)S(1)} %get-tuple-element.11.wu_ref, f32[192,512]{1,0:T(8,128)S(1)} %get-tuple-element.12.gate_ref, ...), custom_call_target="tpu_custom_call" | custom-call | tf_op jit(solution)/shard_map/pallas_call | solution.py:336
  58.2 0.1 collective-permute-start.1
  58.4 0.0 copy-done.3
  58.4 0.0 copy-done.4
  58.4 0.7 shard_map.134.weigh_ref
  59.1 0.1 copy-done.2
  59.1 0.5 shard_map.135.sum_ref
  59.7 0.0 collective-permute-done.2.wd_ref
  59.7 0.1 collective-permute-done.1.hidden_ref
  59.8 0.9 shard_map.136
  60.7 27.9 %all_to_all.10 = bf16[64,8,768]{2,1,0:T(8,128)(2,1)S(1)} all-to-all(bf16[64,8,768]{2,1,0:T(8,128)(2,1)S(1)} %bitcast.8), channel_id=1, replica_groups=mesh['groups'=2,'expert'=64,'tensor'=2] {'expert'}, dimensions={0} | all-to-all | bytes 1572864 | tf_op jit(solution)/shard_map/all_to_all | solution.py:312
  88.7 0.5 shard_map.137
  89.1 2.6 %collective-permute-start.3 = (bf16[16,1792]{1,0:T(8,128)(2,1)S(1)}, bf16[16,1792]{1,0:T(8,128)(2,1)S(1)}, u32[]{:S(2)}, u32[]{:S(2)}) collective-permute-start(bf16[16,1792]{1,0:T(8,128)(2,1)S(1)} %get-tuple-element.16), channel_id=1, source_target_pairs={{0,1},{1,0},{2,3},{3,2},{4,5},{5,4},{6,7},{7,6},{8,9},{9,8},{10,11... | collective-permute-start | bytes 172040 | tf_op jit(solution)/shard_map/ppermute | solution.py:368
  91.7 0.6 copy.14
  92.3 0.3 collective-permute-done.3
  92.6 0.7 maximum_select_fusion
Async XLA Ops:
  4.4 1.3 %copy-start.5 = (bf16[512,1792]{1,0:T(8,128)(2,1)}, bf16[512,1792]{1,0:T(8,128)(2,1)S(1)}, u32[]{:S(2)}) copy-start(bf16[512,1792]{1,0:T(8,128)(2,1)S(1)} %get-tuple-element.14) | copy-start | bytes 5505028
  5.7 38.7 %all-to-all-start = ((bf16[64,8,768]{2,1,0:T(8,128)(2,1)}), bf16[64,8,768]{2,1,0:T(8,128)(2,1)S(1)}, u32[]{:S(2)}, u32[]{:S(2)}) async-start(bf16[64,8,768]{2,1,0:T(8,128)(2,1)} %bitcast.1), calls=%async_computation | async-start | bytes 1572864 | tf_op jit(solution)/shard_map/all_to_all | solution.py:312
  27.5 32.2 %collective-permute-start.2 = (bf16[512,1792]{1,0:T(8,128)(2,1)}, bf16[512,1792]{1,0:T(8,128)(2,1)S(1)}, u32[]{:S(2)}, u32[]{:S(2)}) collective-permute-start(bf16[512,1792]{1,0:T(8,128)(2,1)} %copy-done.5), channel_id=1, source_target_pairs={{0,1},{1,0},{2,3},{3,2},{4,5},{5,4},{6,7},{7,6},{8,9},{9,8},{10,11... | collective-permute-start | bytes 5505032 | tf_op jit(solution)/shard_map/ppermute | solution.py:327
  44.5 12.5 %collective-permute-start = (bf16[512,768]{1,0:T(8,128)(2,1)S(1)}, bf16[512,768]{1,0:T(8,128)(2,1)S(1)}, u32[]{:S(2)}, u32[]{:S(2)}) collective-permute-start(bf16[512,768]{1,0:T(8,128)(2,1)S(1)} %bitcast.10), channel_id=1, source_target_pairs={{0,1},{1,0},{2,3},{3,2},{4,5},{5,4},{6,7},{7,6},{8,9},{9,8},{10,11... | collective-permute-start | bytes 2359304 | tf_op jit(solution)/shard_map/ppermute | solution.py:326
  51.9 2.0 %copy-start = (bf16[1,3584,512]{2,1,0:T(8,128)(2,1)S(1)}, bf16[1,3584,512]{2,1,0:T(8,128)(2,1)}, u32[]{:S(2)}) copy-start(bf16[1,3584,512]{2,1,0:T(8,128)(2,1)} %wg_ref.3) | copy-start | bytes 11010052
  53.9 3.1 %copy-start.1 = (bf16[1,3584,512]{2,1,0:T(8,128)(2,1)S(1)}, bf16[1,3584,512]{2,1,0:T(8,128)(2,1)}, u32[]{:S(2)}) copy-start(bf16[1,3584,512]{2,1,0:T(8,128)(2,1)} %wg_ref.3) | copy-start | bytes 11010052
  57.1 1.3 %copy-start.3 = (s32[16,8]{0,1:T(8,128)S(1)}, s32[16,8]{0,1:T(8,128)}, u32[]{:S(2)}) copy-start(s32[16,8]{0,1:T(8,128)} %param.14) | copy-start | bytes 1540
  57.1 1.3 %copy-start.4 = (s32[16,8]{0,1:T(8,128)S(1)}, s32[16,8]{0,1:T(8,128)}, u32[]{:S(2)}) copy-start(s32[16,8]{0,1:T(8,128)} %param.15) | copy-start | bytes 1540
  57.1 2.1 %copy-start.2 = (bf16[1,512,3584]{2,1,0:T(8,128)(2,1)S(1)}, bf16[1,512,3584]{2,1,0:T(8,128)(2,1)}, u32[]{:S(2)}) copy-start(bf16[1,512,3584]{2,1,0:T(8,128)(2,1)} %wd_ref.1) | copy-start | bytes 11010052
  58.2 1.6 %collective-permute-start.1 = (bf16[192,512]{1,0:T(8,128)(2,1)S(1)}, bf16[192,512]{1,0:T(8,128)(2,1)S(1)}, u32[]{:S(2)}, u32[]{:S(2)}) collective-permute-start(bf16[192,512]{1,0:T(8,128)(2,1)S(1)} %shard_map.133.hidden_ref), channel_id=1, source_target_pairs={{0,1},{1,0},{2,3},{3,2},{4,5},{5,4},{6,7},{7,6},{8,9},{9,8},{10,11... | collective-permute-start | bytes 589832 | tf_op jit(solution)/shard_map/ppermute | solution.py:342
  89.1 3.5 %collective-permute-start.3 = (bf16[16,1792]{1,0:T(8,128)(2,1)S(1)}, bf16[16,1792]{1,0:T(8,128)(2,1)S(1)}, u32[]{:S(2)}, u32[]{:S(2)}) collective-permute-start(bf16[16,1792]{1,0:T(8,128)(2,1)S(1)} %get-tuple-element.16), channel_id=1, source_target_pairs={{0,1},{1,0},{2,3},{3,2},{4,5},{5,4},{6,7},{7,6},{8,9},{9,8},{10,11... | collective-permute-start | bytes 172040 | tf_op jit(solution)/shard_map/ppermute | solution.py:368

commit v6 on v5

--- a/solution.py
+++ b/solution.py
@@ -12,6 +12,7 @@
 softmax_scale = 192.0 ** (-0.5)
 gate_denominator = 1024.0
 BLOCKS = 2
+PACK_COST = pl.CostEstimate(flops=20_000_000_000, bytes_accessed=16_000_000, transcendentals=0)
 
 
 def iota(shape, dim):
@@ -145,17 +146,10 @@
     return copies
 
 
-def own_kernel(
-    own_ref, wg_ref, wu_hbm,
-    gate_ref, upper_ref, attn_ref, next_up_ref,
-    wu, rows, sems,
-):
+def own_kernel(own_ref, wg_ref, wu_ref, gate_ref, upper_ref, attn_ref, rows):
     half = rows.shape[1]
     lat = attn_ref.shape[1]
-    tensor = lax.axis_index("tensor")
-    mine = pl.ds(pl.multiple_of(tensor * half, half), half)
-    theirs = pl.ds(pl.multiple_of((1 - tensor) * half, half), half)
-    copies = copied(((wu_hbm.at[0, mine, :], wu), (wu_hbm.at[0, theirs, :], next_up_ref)), sems)
+    mine = pl.ds(pl.multiple_of(lax.axis_index("tensor") * half, half), half)
     arrived = sort_rows(own_ref[...], rows)
     stats = [arrived[:, lat + k : lat + k + 1] for k in range(6)]
     top = stats[0] + stats[1] + stats[2]
@@ -165,9 +159,7 @@
     done = weighted / jnp.sum(share, axis=0, keepdims=True)
     attn_ref[...] = jnp.broadcast_to(done, attn_ref.shape).astype(bf16)
     gate_ref[...] = dot(rows[...], wg_ref[0, mine, :])
-    copies[0].wait()
-    upper_ref[...] = dot(rows[...], wu[...])
-    copies[1].wait()
+    upper_ref[...] = dot(rows[...], wu_ref[0, mine, :])
 
 
 def other_kernel(other_ref, wg_ref, wu_ref, gate_ref, upper_ref, hidden_ref, rows):
@@ -175,7 +167,7 @@
     theirs = pl.ds(pl.multiple_of((1 - lax.axis_index("tensor")) * half, half), half)
     sort_rows(other_ref[...], rows)
     gate = gate_ref[...] + dot(rows[...], wg_ref[0, theirs, :])
-    upper = upper_ref[...] + dot(rows[...], wu_ref[...])
+    upper = upper_ref[...] + dot(rows[...], wu_ref[0, theirs, :])
     hidden_ref[...] = (gate / (1.0 + jnp.exp(-gate)) * upper).astype(bf16)
 
 
@@ -270,7 +262,7 @@
     return [pltpu.with_memory_space_constraint(a, pltpu.VMEM) for a in arrays]
 
 
-def call(kernel, out_shape, in_specs, scratch=(), vmem_mib=32):
+def call(kernel, out_shape, in_specs, scratch=(), vmem_mib=32, cost=None):
     several = isinstance(out_shape, (tuple, list))
     return pl.pallas_call(
         kernel,
@@ -279,6 +271,7 @@
         out_specs=tuple(vmem() for _ in out_shape) if several else vmem(),
         scratch_shapes=list(scratch),
         compiler_params=pltpu.CompilerParams(vmem_limit_bytes=vmem_mib << 20),
+        cost_estimate=cost,
     )
 
 
@@ -321,24 +314,24 @@
         [pltpu.SMEM(ctx_len.shape, ctx_len.dtype)]
         + [pltpu.VMEM(a.shape, a.dtype) for a in arrays]
         + [pltpu.SemaphoreType.DMA((8,))],
+        cost=PACK_COST,
     )(batch_len, *in_hbm(ctx_len, *arrays, w_down))
     own = exchanged(packed)
     other = lax.ppermute(own, "tensor", swap)
     down_other = lax.ppermute(given, "tensor", swap)
     partial = jax.ShapeDtypeStruct((slots, hidden_units), f32)
-    half_up = pltpu.VMEM((half, hidden_units), bf16)
-    gate, upper, attn, next_up = call(
+    gate, upper, attn = call(
         own_kernel,
-        (partial, partial, jax.ShapeDtypeStruct((16, lat), bf16), half_up),
-        [vmem(), vmem(), hbm()],
-        [half_up, pltpu.VMEM((slots, half), bf16), pltpu.SemaphoreType.DMA((2,))],
-    )(own, w_gate, *in_hbm(w_up))
+        (partial, partial, jax.ShapeDtypeStruct((16, lat), bf16)),
+        [vmem(), vmem(), vmem()],
+        [pltpu.VMEM((slots, half), bf16)],
+    )(own, w_gate, w_up)
     hidden = call(
         other_kernel,
         jax.ShapeDtypeStruct((slots, hidden_units), bf16),
         [vmem() for _ in range(5)],
         [pltpu.VMEM((slots, half), bf16)],
-    )(other, w_gate, *in_vmem(next_up), gate, upper)
+    )(other, w_gate, w_up, gate, upper)
     hidden_other = lax.ppermute(hidden, "tensor", swap)
     weights = call(
         weigh_kernel,

time: 93.6 us -> 95.7 us (1.022)
  local copies, waits for them, and re-layouts: 4.13 us -> 8.05 us
  Pallas kernels: 9.89 us -> 8.04 us
    unnamed x13 -> x17, local copies, waits for them, and re-layouts: 4.13 us -> 8.05 us
    pallas_call x1, Pallas kernels: 3 us -> 1.13 us  [local(): call(own_kernel, (partial, partial, jax.ShapeDtypeStruct((16, lat), bf16)...]
  transfers between devices with their start and end apart: 5 -> 5, of which waited for: 3 -> 3; matrix products, arithmetic and copies ran while one was open for 1% -> 1% of each run, Pallas kernels for 6% -> 4%
where the time goes in v6:
time: 95.7 us; the launch traced here: 95.4 us
  starting transfers between devices  37.2 us (39%)
  blocking collectives  27.9 us (29%)
  waiting for transfers between devices  12 us (13%)
  local copies, waits for them, and re-layouts  8.05 us (8%)
  Pallas kernels  8.04 us (8%)
  between operations  1.39 us (1%)
    all_to_all x1, blocking collectives, exchanged(): lax.all_to_all(whole, 'expert', 0, 0, tiled=True).reshape(total_rows, width)  27.9 us
    all_to_all x1, starting transfers between devices, exchanged(): lax.all_to_all(whole, 'expert', 0, 0, tiled=True).reshape(total_rows, width)  21.8 us
    all_to_all x1, waiting for transfers between devices, exchanged(): lax.all_to_all(whole, 'expert', 0, 0, tiled=True).reshape(total_rows, width)  11.7 us
    unnamed x17, local copies, waits for them, and re-layouts  8.05 us
    ppermute x1, starting transfers between devices, local(): other = lax.ppermute(own, 'tensor', swap)  7.43 us
    ppermute x1, starting transfers between devices, local(): down_other = lax.ppermute(given, 'tensor', swap)  5.23 us
    pallas_call x1, Pallas kernels, local(): call(pack_kernel, (pltpu.VMEM((total_rows, width), bf16), half_down), [sm...  3.18 us
    ppermute x1, starting transfers between devices, local(): moe_other = lax.ppermute(moe_half, 'tensor', swap)  2.6 us
  transfers between devices with their start and end apart: 5, of which 3 were waited for; matrix products, arithmetic and copies ran while one was open for 1% of the time, Pallas kernels for 4%

profile of v6, /device:TPU:513, one launch (start us, length us, event | category | flops | bytes accessed | tf_op | source)
XLA Modules:
  0.0 95.4 jit_solution(491620505044462908)
XLA Ops:
  1.3 3.2 %shard_map.131 = (bf16[512,768]{1,0:T(8,128)(2,1)}, bf16[512,1792]{1,0:T(8,128)(2,1)S(1)}) custom-call(s32[1]{0:T(128)S(6)} %copy.15.len_ref, s32[2]{0:T(128)} %ctx_hbm.1, bf16[16,3584]{1,0:T(8,128)(2,1)} %hid_hbm.1, s32[8,16]{1,0:T(8,128)} %bitcast.12, bf16[2,32,512]{2,1,0:T(8,128)(2,1)} %ql_hbm.1, bf16[2,32,64]{2,1,0:T(8,128)(2,1)} %qr_hbm.1, ...), custom_call_target="tpu_custom_call" | custom-call | flops 20000000000 | bytes 16000000 | tf_op jit(solution)/shard_map/pallas_call | solution.py:310
  4.5 0.0 copy-start.7
  4.5 1.3 %copy-done.7 = bf16[512,1792]{1,0:T(8,128)(2,1)} copy-done((bf16[512,1792]{1,0:T(8,128)(2,1)}, bf16[512,1792]{1,0:T(8,128)(2,1)S(1)}, u32[]{:S(2)}) %copy-start.7) | copy-done | bytes 1835032
  5.7 21.8 %all-to-all-start = ((bf16[64,8,768]{2,1,0:T(8,128)(2,1)}), bf16[64,8,768]{2,1,0:T(8,128)(2,1)S(1)}, u32[]{:S(2)}, u32[]{:S(2)}) async-start(bf16[64,8,768]{2,1,0:T(8,128)(2,1)} %bitcast.1), calls=%async_computation | async-start | bytes 1572864 | tf_op jit(solution)/shard_map/all_to_all | solution.py:305
  27.5 5.2 %collective-permute-start.2 = (bf16[512,1792]{1,0:T(8,128)(2,1)}, bf16[512,1792]{1,0:T(8,128)(2,1)S(1)}, u32[]{:S(2)}, u32[]{:S(2)}) collective-permute-start(bf16[512,1792]{1,0:T(8,128)(2,1)} %copy-done.7), channel_id=1, source_target_pairs={{0,1},{1,0},{2,3},{3,2},{4,5},{5,4},{6,7},{7,6},{8,9},{9,8},{10,11... | collective-permute-start | bytes 5505032 | tf_op jit(solution)/shard_map/ppermute | solution.py:321
  32.8 11.7 %all-to-all-done = bf16[64,8,768]{2,1,0:T(8,128)(2,1)S(1)} async-done(((bf16[64,8,768]{2,1,0:T(8,128)(2,1)}), bf16[64,8,768]{2,1,0:T(8,128)(2,1)S(1)}, u32[]{:S(2)}, u32[]{:S(2)}) %all-to-all-start) | async-done | bytes 786464 | tf_op jit(solution)/shard_map/all_to_all | solution.py:305
  44.5 7.4 %collective-permute-start = (bf16[512,768]{1,0:T(8,128)(2,1)S(1)}, bf16[512,768]{1,0:T(8,128)(2,1)S(1)}, u32[]{:S(2)}, u32[]{:S(2)}) collective-permute-start(bf16[512,768]{1,0:T(8,128)(2,1)S(1)} %bitcast.10), channel_id=1, source_target_pairs={{0,1},{1,0},{2,3},{3,2},{4,5},{5,4},{6,7},{7,6},{8,9},{9,8},{10,11... | collective-permute-start | bytes 2359304 | tf_op jit(solution)/shard_map/ppermute | solution.py:320
  51.9 0.0 copy-start
  51.9 2.0 %copy-done = bf16[1,3584,512]{2,1,0:T(8,128)(2,1)S(1)} copy-done((bf16[1,3584,512]{2,1,0:T(8,128)(2,1)S(1)}, bf16[1,3584,512]{2,1,0:T(8,128)(2,1)}, u32[]{:S(2)}) %copy-start) | copy-done | bytes 3670040
  53.9 0.0 copy-start.2
  54.0 2.0 %copy-done.2 = bf16[1,3584,512]{2,1,0:T(8,128)(2,1)S(1)} copy-done((bf16[1,3584,512]{2,1,0:T(8,128)(2,1)S(1)}, bf16[1,3584,512]{2,1,0:T(8,128)(2,1)}, u32[]{:S(2)}) %copy-start.2) | copy-done | bytes 3670040
  56.0 0.0 copy-start.1
  56.0 0.0 copy-start.3
  56.0 1.1 %shard_map.132 = (f32[192,512]{1,0:T(8,128)S(1)}, f32[192,512]{1,0:T(8,128)S(1)}, bf16[16,512]{1,0:T(8,128)(2,1)S(1)}) custom-call(bf16[512,768]{1,0:T(8,128)(2,1)S(1)} %bitcast.11, bf16[1,3584,512]{2,1,0:T(8,128)(2,1)S(1)} %copy-done, bf16[1,3584,512]{2,1,0:T(8,128)(2,1)S(1)} %copy-done.2), custom_call_target="tpu_custom_call" | custom-call | tf_op jit(solution)/shard_map/pallas_call | solution.py:323
  57.1 0.0 collective-permute-done.other_ref
  57.1 0.9 copy-done.1
  58.0 1.1 %copy-done.3 = bf16[1,3584,512]{2,1,0:T(8,128)(2,1)S(1)} copy-done((bf16[1,3584,512]{2,1,0:T(8,128)(2,1)S(1)}, bf16[1,3584,512]{2,1,0:T(8,128)(2,1)}, u32[]{:S(2)}) %copy-start.3) | copy-done | bytes 3670040
  59.1 0.0 copy-start.5
  59.1 0.0 copy-start.6
  59.1 0.0 copy-start.4
  59.2 1.1 %shard_map.133.hidden_ref = bf16[192,512]{1,0:T(8,128)(2,1)S(1)} custom-call(bf16[512,768]{1,0:T(8,128)(2,1)S(1)} %collective-permute-done.other_ref, bf16[1,3584,512]{2,1,0:T(8,128)(2,1)S(1)} %copy-done.1, bf16[1,3584,512]{2,1,0:T(8,128)(2,1)S(1)} %copy-done.3, f32[192,512]{1,0:T(8,128)S(1)} %get-tuple-element.10.gate_ref, ...), custom_call_target="tpu_custom_call" | custom-call | tf_op jit(solution)/shard_map/pallas_call | solution.py:329
  60.3 0.1 collective-permute-start.1
  60.4 0.0 copy-done.5
  60.5 0.0 copy-done.6
  60.5 0.7 shard_map.134.weigh_ref
  61.1 0.1 copy-done.4
  61.2 0.5 shard_map.135.sum_ref
  61.8 0.0 collective-permute-done.2.wd_ref
  61.8 0.1 collective-permute-done.1.hidden_ref
  61.9 0.9 shard_map.136
  62.8 27.9 %all_to_all.10 = bf16[64,8,768]{2,1,0:T(8,128)(2,1)S(1)} all-to-all(bf16[64,8,768]{2,1,0:T(8,128)(2,1)S(1)} %bitcast.8), channel_id=1, replica_groups=mesh['groups'=2,'expert'=64,'tensor'=2] {'expert'}, dimensions={0} | all-to-all | bytes 1572864 | tf_op jit(solution)/shard_map/all_to_all | solution.py:305
  90.7 0.5 shard_map.137
  91.2 2.6 %collective-permute-start.3 = (bf16[16,1792]{1,0:T(8,128)(2,1)S(1)}, bf16[16,1792]{1,0:T(8,128)(2,1)S(1)}, u32[]{:S(2)}, u32[]{:S(2)}) collective-permute-start(bf16[16,1792]{1,0:T(8,128)(2,1)S(1)} %get-tuple-element.14), channel_id=1, source_target_pairs={{0,1},{1,0},{2,3},{3,2},{4,5},{5,4},{6,7},{7,6},{8,9},{9,8},{10,11... | collective-permute-start | bytes 172040 | tf_op jit(solution)/shard_map/ppermute | solution.py:361
  93.8 0.6 copy.14
  94.4 0.3 collective-permute-done.3
  94.7 0.7 maximum_select_fusion
Async XLA Ops:
  4.5 1.3 %copy-start.7 = (bf16[512,1792]{1,0:T(8,128)(2,1)}, bf16[512,1792]{1,0:T(8,128)(2,1)S(1)}, u32[]{:S(2)}) copy-start(bf16[512,1792]{1,0:T(8,128)(2,1)S(1)} %get-tuple-element.12) | copy-start | bytes 5505028
  5.7 38.7 %all-to-all-start = ((bf16[64,8,768]{2,1,0:T(8,128)(2,1)}), bf16[64,8,768]{2,1,0:T(8,128)(2,1)S(1)}, u32[]{:S(2)}, u32[]{:S(2)}) async-start(bf16[64,8,768]{2,1,0:T(8,128)(2,1)} %bitcast.1), calls=%async_computation | async-start | bytes 1572864 | tf_op jit(solution)/shard_map/all_to_all | solution.py:305
  27.5 34.2 %collective-permute-start.2 = (bf16[512,1792]{1,0:T(8,128)(2,1)}, bf16[512,1792]{1,0:T(8,128)(2,1)S(1)}, u32[]{:S(2)}, u32[]{:S(2)}) collective-permute-start(bf16[512,1792]{1,0:T(8,128)(2,1)} %copy-done.7), channel_id=1, source_target_pairs={{0,1},{1,0},{2,3},{3,2},{4,5},{5,4},{6,7},{7,6},{8,9},{9,8},{10,11... | collective-permute-start | bytes 5505032 | tf_op jit(solution)/shard_map/ppermute | solution.py:321
  44.5 12.7 %collective-permute-start = (bf16[512,768]{1,0:T(8,128)(2,1)S(1)}, bf16[512,768]{1,0:T(8,128)(2,1)S(1)}, u32[]{:S(2)}, u32[]{:S(2)}) collective-permute-start(bf16[512,768]{1,0:T(8,128)(2,1)S(1)} %bitcast.10), channel_id=1, source_target_pairs={{0,1},{1,0},{2,3},{3,2},{4,5},{5,4},{6,7},{7,6},{8,9},{9,8},{10,11... | collective-permute-start | bytes 2359304 | tf_op jit(solution)/shard_map/ppermute | solution.py:320
  51.9 2.0 %copy-start = (bf16[1,3584,512]{2,1,0:T(8,128)(2,1)S(1)}, bf16[1,3584,512]{2,1,0:T(8,128)(2,1)}, u32[]{:S(2)}) copy-start(bf16[1,3584,512]{2,1,0:T(8,128)(2,1)} %wg_ref.3) | copy-start | bytes 11010052
  53.9 2.0 %copy-start.2 = (bf16[1,3584,512]{2,1,0:T(8,128)(2,1)S(1)}, bf16[1,3584,512]{2,1,0:T(8,128)(2,1)}, u32[]{:S(2)}) copy-start(bf16[1,3584,512]{2,1,0:T(8,128)(2,1)} %wu_ref.3) | copy-start | bytes 11010052
  56.0 2.0 %copy-start.1 = (bf16[1,3584,512]{2,1,0:T(8,128)(2,1)S(1)}, bf16[1,3584,512]{2,1,0:T(8,128)(2,1)}, u32[]{:S(2)}) copy-start(bf16[1,3584,512]{2,1,0:T(8,128)(2,1)} %wg_ref.3) | copy-start | bytes 11010052
  56.0 3.2 %copy-start.3 = (bf16[1,3584,512]{2,1,0:T(8,128)(2,1)S(1)}, bf16[1,3584,512]{2,1,0:T(8,128)(2,1)}, u32[]{:S(2)}) copy-start(bf16[1,3584,512]{2,1,0:T(8,128)(2,1)} %wu_ref.3) | copy-start | bytes 11010052
  59.1 1.3 %copy-start.5 = (s32[16,8]{0,1:T(8,128)S(1)}, s32[16,8]{0,1:T(8,128)}, u32[]{:S(2)}) copy-start(s32[16,8]{0,1:T(8,128)} %param.14) | copy-start | bytes 1540
  59.1 1.3 %copy-start.6 = (s32[16,8]{0,1:T(8,128)S(1)}, s32[16,8]{0,1:T(8,128)}, u32[]{:S(2)}) copy-start(s32[16,8]{0,1:T(8,128)} %param.15) | copy-start | bytes 1540
  59.1 2.1 %copy-start.4 = (bf16[1,512,3584]{2,1,0:T(8,128)(2,1)S(1)}, bf16[1,512,3584]{2,1,0:T(8,128)(2,1)}, u32[]{:S(2)}) copy-start(bf16[1,512,3584]{2,1,0:T(8,128)(2,1)} %wd_ref.1) | copy-start | bytes 11010052
  60.3 1.6 %collective-permute-start.1 = (bf16[192,512]{1,0:T(8,128)(2,1)S(1)}, bf16[192,512]{1,0:T(8,128)(2,1)S(1)}, u32[]{:S(2)}, u32[]{:S(2)}) collective-permute-start(bf16[192,512]{1,0:T(8,128)(2,1)S(1)} %shard_map.133.hidden_ref), channel_id=1, source_target_pairs={{0,1},{1,0},{2,3},{3,2},{4,5},{5,4},{6,7},{7,6},{8,9},{9,8},{10,11... | collective-permute-start | bytes 589832 | tf_op jit(solution)/shard_map/ppermute | solution.py:335
  91.2 3.5 %collective-permute-start.3 = (bf16[16,1792]{1,0:T(8,128)(2,1)S(1)}, bf16[16,1792]{1,0:T(8,128)(2,1)S(1)}, u32[]{:S(2)}, u32[]{:S(2)}) collective-permute-start(bf16[16,1792]{1,0:T(8,128)(2,1)S(1)} %get-tuple-element.14), channel_id=1, source_target_pairs={{0,1},{1,0},{2,3},{3,2},{4,5},{5,4},{6,7},{7,6},{8,9},{9,8},{10,11... | collective-permute-start | bytes 172040 | tf_op jit(solution)/shard_map/ppermute | solution.py:361

commit v7 on v6

--- a/solution.py
+++ b/solution.py
@@ -162,7 +162,7 @@
     upper_ref[...] = dot(rows[...], wu_ref[0, mine, :])
 
 
-def other_kernel(other_ref, wg_ref, wu_ref, gate_ref, upper_ref, hidden_ref, rows):
+def other_kernel(other_ref, wg_ref, wu_ref, gate_ref, upper_ref, weigh_ref, hidden_ref, rows):
     half = rows.shape[1]
     theirs = pl.ds(pl.multiple_of((1 - lax.axis_index("tensor")) * half, half), half)
     sort_rows(other_ref[...], rows)
@@ -171,11 +171,11 @@
     hidden_ref[...] = (gate / (1.0 + jnp.exp(-gate)) * upper).astype(bf16)
 
 
-def weigh_kernel(hidden_ref, len_ref, ids_ref, gate_ref, weigh_ref):
+def weigh_kernel(after_ref, len_ref, ids_ref, gate_ref, weigh_ref):
     weigh(len_ref, ids_ref, gate_ref, weigh_ref)
 
 
-def down_kernel(hidden_ref, wd_ref, weigh_ref, sum_ref):
+def down_kernel(hidden_ref, wd_ref, sum_ref):
     half = sum_ref.shape[1]
     mine = pl.ds(pl.multiple_of(lax.axis_index("tensor") * half, half), half)
     sum_ref[...] = dot(hidden_ref[...], wd_ref[0, :, mine])
@@ -326,23 +326,23 @@
         [vmem(), vmem(), vmem()],
         [pltpu.VMEM((slots, half), bf16)],
     )(own, w_gate, w_up)
-    hidden = call(
-        other_kernel,
-        jax.ShapeDtypeStruct((slots, hidden_units), bf16),
-        [vmem() for _ in range(5)],
-        [pltpu.VMEM((slots, half), bf16)],
-    )(other, w_gate, w_up, gate, upper)
-    hidden_other = lax.ppermute(hidden, "tensor", swap)
     weights = call(
         weigh_kernel,
         jax.ShapeDtypeStruct((2 * CAP, SUB * tok, total_rows), bf16),
         [vmem(), smem(), vmem(), vmem()],
-    )(hidden, batch_len, ids_t, gate_t)
+    )(gate, batch_len, ids_t, gate_t)
+    hidden = call(
+        other_kernel,
+        jax.ShapeDtypeStruct((slots, hidden_units), bf16),
+        [vmem() for _ in range(6)],
+        [pltpu.VMEM((slots, half), bf16)],
+    )(other, w_gate, w_up, gate, upper, weights)
+    hidden_other = lax.ppermute(hidden, "tensor", swap)
     summed = call(
         down_kernel,
         jax.ShapeDtypeStruct((slots, half), f32),
-        [vmem(), vmem(), vmem()],
-    )(hidden, w_down, weights)
+        [vmem(), vmem()],
+    )(hidden, w_down)
     returned = call(
         back_kernel,
         jax.ShapeDtypeStruct((total_rows, width), bf16),

time: 95.7 us -> 95.8 us (level)
  no operation moved by 1% of the time
where the time goes in v7:
time: 95.8 us; the launch traced here: 95.5 us
  starting transfers between devices  37.3 us (39%)
  blocking collectives  27.9 us (29%)
  waiting for transfers between devices  12.1 us (13%)
  Pallas kernels  8.06 us (8%)
  local copies, waits for them, and re-layouts  8.04 us (8%)
  between operations  1.4 us (1%)
    all_to_all x1, blocking collectives, exchanged(): lax.all_to_all(whole, 'expert', 0, 0, tiled=True).reshape(total_rows, width)  27.9 us
    all_to_all x1, starting transfers between devices, exchanged(): lax.all_to_all(whole, 'expert', 0, 0, tiled=True).reshape(total_rows, width)  21.8 us
    all_to_all x1, waiting for transfers between devices, exchanged(): lax.all_to_all(whole, 'expert', 0, 0, tiled=True).reshape(total_rows, width)  11.7 us
    unnamed x17, local copies, waits for them, and re-layouts  8.04 us
    ppermute x1, starting transfers between devices, local(): other = lax.ppermute(own, 'tensor', swap)  7.43 us
    ppermute x1, starting transfers between devices, local(): down_other = lax.ppermute(given, 'tensor', swap)  5.23 us
    pallas_call x1, Pallas kernels, local(): call(pack_kernel, (pltpu.VMEM((total_rows, width), bf16), half_down), [sm...  3.18 us
    ppermute x1, starting transfers between devices, local(): moe_other = lax.ppermute(moe_half, 'tensor', swap)  2.69 us
  transfers between devices with their start and end apart: 5, of which 3 were waited for; matrix products, arithmetic and copies ran while one was open for 1% of the time, Pallas kernels for 4%

profile of v7, /device:TPU:513, one launch (start us, length us, event | category | flops | bytes accessed | tf_op | source)
XLA Modules:
  0.0 95.5 jit_solution(2080698560165738301)
XLA Ops:
  1.3 3.2 %shard_map.131 = (bf16[512,768]{1,0:T(8,128)(2,1)}, bf16[512,1792]{1,0:T(8,128)(2,1)S(1)}) custom-call(s32[1]{0:T(128)S(6)} %copy.15.len_ref, s32[2]{0:T(128)} %ctx_hbm.1, bf16[16,3584]{1,0:T(8,128)(2,1)} %hid_hbm.1, s32[8,16]{1,0:T(8,128)} %bitcast.12, bf16[2,32,512]{2,1,0:T(8,128)(2,1)} %ql_hbm.1, bf16[2,32,64]{2,1,0:T(8,128)(2,1)} %qr_hbm.1, ...), custom_call_target="tpu_custom_call" | custom-call | flops 20000000000 | bytes 16000000 | tf_op jit(solution)/shard_map/pallas_call | solution.py:310
  4.5 0.0 copy-start.7
  4.5 1.3 %copy-done.7 = bf16[512,1792]{1,0:T(8,128)(2,1)} copy-done((bf16[512,1792]{1,0:T(8,128)(2,1)}, bf16[512,1792]{1,0:T(8,128)(2,1)S(1)}, u32[]{:S(2)}) %copy-start.7) | copy-done | bytes 1835032
  5.7 21.8 %all-to-all-start = ((bf16[64,8,768]{2,1,0:T(8,128)(2,1)}), bf16[64,8,768]{2,1,0:T(8,128)(2,1)S(1)}, u32[]{:S(2)}, u32[]{:S(2)}) async-start(bf16[64,8,768]{2,1,0:T(8,128)(2,1)} %bitcast.1), calls=%async_computation | async-start | bytes 1572864 | tf_op jit(solution)/shard_map/all_to_all | solution.py:305
  27.5 5.2 %collective-permute-start.2 = (bf16[512,1792]{1,0:T(8,128)(2,1)}, bf16[512,1792]{1,0:T(8,128)(2,1)S(1)}, u32[]{:S(2)}, u32[]{:S(2)}) collective-permute-start(bf16[512,1792]{1,0:T(8,128)(2,1)} %copy-done.7), channel_id=1, source_target_pairs={{0,1},{1,0},{2,3},{3,2},{4,5},{5,4},{6,7},{7,6},{8,9},{9,8},{10,11... | collective-permute-start | bytes 5505032 | tf_op jit(solution)/shard_map/ppermute | solution.py:321
  32.8 11.7 %all-to-all-done = bf16[64,8,768]{2,1,0:T(8,128)(2,1)S(1)} async-done(((bf16[64,8,768]{2,1,0:T(8,128)(2,1)}), bf16[64,8,768]{2,1,0:T(8,128)(2,1)S(1)}, u32[]{:S(2)}, u32[]{:S(2)}) %all-to-all-start) | async-done | bytes 786464 | tf_op jit(solution)/shard_map/all_to_all | solution.py:305
  44.5 7.4 %collective-permute-start = (bf16[512,768]{1,0:T(8,128)(2,1)S(1)}, bf16[512,768]{1,0:T(8,128)(2,1)S(1)}, u32[]{:S(2)}, u32[]{:S(2)}) collective-permute-start(bf16[512,768]{1,0:T(8,128)(2,1)S(1)} %bitcast.10), channel_id=1, source_target_pairs={{0,1},{1,0},{2,3},{3,2},{4,5},{5,4},{6,7},{7,6},{8,9},{9,8},{10,11... | collective-permute-start | bytes 2359304 | tf_op jit(solution)/shard_map/ppermute | solution.py:320
  51.9 0.0 copy-start
  51.9 2.0 %copy-done = bf16[1,3584,512]{2,1,0:T(8,128)(2,1)S(1)} copy-done((bf16[1,3584,512]{2,1,0:T(8,128)(2,1)S(1)}, bf16[1,3584,512]{2,1,0:T(8,128)(2,1)}, u32[]{:S(2)}) %copy-start) | copy-done | bytes 3670040
  53.9 0.0 copy-start.2
  54.0 2.0 %copy-done.2 = bf16[1,3584,512]{2,1,0:T(8,128)(2,1)S(1)} copy-done((bf16[1,3584,512]{2,1,0:T(8,128)(2,1)S(1)}, bf16[1,3584,512]{2,1,0:T(8,128)(2,1)}, u32[]{:S(2)}) %copy-start.2) | copy-done | bytes 3670040
  56.0 0.0 copy-start.5
  56.0 0.0 copy-start.6
  56.0 0.0 copy-start.1
  56.0 0.0 copy-start.3
  56.0 1.1 %shard_map.132 = (f32[192,512]{1,0:T(8,128)S(1)}, f32[192,512]{1,0:T(8,128)S(1)}, bf16[16,512]{1,0:T(8,128)(2,1)S(1)}) custom-call(bf16[512,768]{1,0:T(8,128)(2,1)S(1)} %bitcast.11, bf16[1,3584,512]{2,1,0:T(8,128)(2,1)S(1)} %copy-done, bf16[1,3584,512]{2,1,0:T(8,128)(2,1)S(1)} %copy-done.2), custom_call_target="tpu_custom_call" | custom-call | tf_op jit(solution)/shard_map/pallas_call | solution.py:323
  57.1 0.0 copy-done.5
  57.1 0.0 copy-done.6
  57.2 0.7 shard_map.133.weigh_ref
  57.8 0.0 collective-permute-done.other_ref
  57.9 0.2 copy-done.1
  58.1 1.1 %copy-done.3 = bf16[1,3584,512]{2,1,0:T(8,128)(2,1)S(1)} copy-done((bf16[1,3584,512]{2,1,0:T(8,128)(2,1)S(1)}, bf16[1,3584,512]{2,1,0:T(8,128)(2,1)}, u32[]{:S(2)}) %copy-start.3) | copy-done | bytes 3670040
  59.2 0.0 copy-start.4
  59.2 1.1 %shard_map.134.hidden_ref = bf16[192,512]{1,0:T(8,128)(2,1)S(1)} custom-call(bf16[512,768]{1,0:T(8,128)(2,1)S(1)} %collective-permute-done.other_ref, bf16[1,3584,512]{2,1,0:T(8,128)(2,1)S(1)} %copy-done.1, bf16[1,3584,512]{2,1,0:T(8,128)(2,1)S(1)} %copy-done.3, f32[192,512]{1,0:T(8,128)S(1)} %get-tuple-element.10.after_ref.gate_ref, ...), custom_call_target="tpu_custom_call" | custom-call | tf_op jit(solution)/shard_map/pallas_call | solution.py:334
  60.3 0.1 collective-permute-start.1
  60.5 0.7 copy-done.4
  61.2 0.5 shard_map.135.sum_ref
  61.8 0.0 collective-permute-done.2.wd_ref
  61.8 0.1 collective-permute-done.1.hidden_ref
  61.9 0.9 shard_map.136
  62.8 27.9 %all_to_all.10 = bf16[64,8,768]{2,1,0:T(8,128)(2,1)S(1)} all-to-all(bf16[64,8,768]{2,1,0:T(8,128)(2,1)S(1)} %bitcast.8), channel_id=1, replica_groups=mesh['groups'=2,'expert'=64,'tensor'=2] {'expert'}, dimensions={0} | all-to-all | bytes 1572864 | tf_op jit(solution)/shard_map/all_to_all | solution.py:305
  90.8 0.5 shard_map.137
  91.2 2.7 %collective-permute-start.3 = (bf16[16,1792]{1,0:T(8,128)(2,1)S(1)}, bf16[16,1792]{1,0:T(8,128)(2,1)S(1)}, u32[]{:S(2)}, u32[]{:S(2)}) collective-permute-start(bf16[16,1792]{1,0:T(8,128)(2,1)S(1)} %get-tuple-element.14), channel_id=1, source_target_pairs={{0,1},{1,0},{2,3},{3,2},{4,5},{5,4},{6,7},{7,6},{8,9},{9,8},{10,11... | collective-permute-start | bytes 172040 | tf_op jit(solution)/shard_map/ppermute | solution.py:361
  93.9 0.6 copy.14
  94.5 0.3 collective-permute-done.3
  94.8 0.7 maximum_select_fusion
Async XLA Ops:
  4.5 1.3 %copy-start.7 = (bf16[512,1792]{1,0:T(8,128)(2,1)}, bf16[512,1792]{1,0:T(8,128)(2,1)S(1)}, u32[]{:S(2)}) copy-start(bf16[512,1792]{1,0:T(8,128)(2,1)S(1)} %get-tuple-element.12) | copy-start | bytes 5505028
  5.7 38.7 %all-to-all-start = ((bf16[64,8,768]{2,1,0:T(8,128)(2,1)}), bf16[64,8,768]{2,1,0:T(8,128)(2,1)S(1)}, u32[]{:S(2)}, u32[]{:S(2)}) async-start(bf16[64,8,768]{2,1,0:T(8,128)(2,1)} %bitcast.1), calls=%async_computation | async-start | bytes 1572864 | tf_op jit(solution)/shard_map/all_to_all | solution.py:305
  27.5 34.2 %collective-permute-start.2 = (bf16[512,1792]{1,0:T(8,128)(2,1)}, bf16[512,1792]{1,0:T(8,128)(2,1)S(1)}, u32[]{:S(2)}, u32[]{:S(2)}) collective-permute-start(bf16[512,1792]{1,0:T(8,128)(2,1)} %copy-done.7), channel_id=1, source_target_pairs={{0,1},{1,0},{2,3},{3,2},{4,5},{5,4},{6,7},{7,6},{8,9},{9,8},{10,11... | collective-permute-start | bytes 5505032 | tf_op jit(solution)/shard_map/ppermute | solution.py:321
  44.5 13.4 %collective-permute-start = (bf16[512,768]{1,0:T(8,128)(2,1)S(1)}, bf16[512,768]{1,0:T(8,128)(2,1)S(1)}, u32[]{:S(2)}, u32[]{:S(2)}) collective-permute-start(bf16[512,768]{1,0:T(8,128)(2,1)S(1)} %bitcast.10), channel_id=1, source_target_pairs={{0,1},{1,0},{2,3},{3,2},{4,5},{5,4},{6,7},{7,6},{8,9},{9,8},{10,11... | collective-permute-start | bytes 2359304 | tf_op jit(solution)/shard_map/ppermute | solution.py:320
  51.9 2.0 %copy-start = (bf16[1,3584,512]{2,1,0:T(8,128)(2,1)S(1)}, bf16[1,3584,512]{2,1,0:T(8,128)(2,1)}, u32[]{:S(2)}) copy-start(bf16[1,3584,512]{2,1,0:T(8,128)(2,1)} %wg_ref.3) | copy-start | bytes 11010052
  53.9 2.0 %copy-start.2 = (bf16[1,3584,512]{2,1,0:T(8,128)(2,1)S(1)}, bf16[1,3584,512]{2,1,0:T(8,128)(2,1)}, u32[]{:S(2)}) copy-start(bf16[1,3584,512]{2,1,0:T(8,128)(2,1)} %wu_ref.3) | copy-start | bytes 11010052
  56.0 1.2 %copy-start.5 = (s32[16,8]{0,1:T(8,128)S(1)}, s32[16,8]{0,1:T(8,128)}, u32[]{:S(2)}) copy-start(s32[16,8]{0,1:T(8,128)} %param.14) | copy-start | bytes 1540
  56.0 1.2 %copy-start.6 = (s32[16,8]{0,1:T(8,128)S(1)}, s32[16,8]{0,1:T(8,128)}, u32[]{:S(2)}) copy-start(s32[16,8]{0,1:T(8,128)} %param.15) | copy-start | bytes 1540
  56.0 2.1 %copy-start.1 = (bf16[1,3584,512]{2,1,0:T(8,128)(2,1)S(1)}, bf16[1,3584,512]{2,1,0:T(8,128)(2,1)}, u32[]{:S(2)}) copy-start(bf16[1,3584,512]{2,1,0:T(8,128)(2,1)} %wg_ref.3) | copy-start | bytes 11010052
  56.0 3.2 %copy-start.3 = (bf16[1,3584,512]{2,1,0:T(8,128)(2,1)S(1)}, bf16[1,3584,512]{2,1,0:T(8,128)(2,1)}, u32[]{:S(2)}) copy-start(bf16[1,3584,512]{2,1,0:T(8,128)(2,1)} %wu_ref.3) | copy-start | bytes 11010052
  59.2 2.0 %copy-start.4 = (bf16[1,512,3584]{2,1,0:T(8,128)(2,1)S(1)}, bf16[1,512,3584]{2,1,0:T(8,128)(2,1)}, u32[]{:S(2)}) copy-start(bf16[1,512,3584]{2,1,0:T(8,128)(2,1)} %wd_ref.1) | copy-start | bytes 11010052
  60.3 1.6 %collective-permute-start.1 = (bf16[192,512]{1,0:T(8,128)(2,1)S(1)}, bf16[192,512]{1,0:T(8,128)(2,1)S(1)}, u32[]{:S(2)}, u32[]{:S(2)}) collective-permute-start(bf16[192,512]{1,0:T(8,128)(2,1)S(1)} %shard_map.134.hidden_ref), channel_id=1, source_target_pairs={{0,1},{1,0},{2,3},{3,2},{4,5},{5,4},{6,7},{7,6},{8,9},{9,8},{10,11... | collective-permute-start | bytes 589832 | tf_op jit(solution)/shard_map/ppermute | solution.py:340
  91.2 3.6 %collective-permute-start.3 = (bf16[16,1792]{1,0:T(8,128)(2,1)S(1)}, bf16[16,1792]{1,0:T(8,128)(2,1)S(1)}, u32[]{:S(2)}, u32[]{:S(2)}) collective-permute-start(bf16[16,1792]{1,0:T(8,128)(2,1)S(1)} %get-tuple-element.14), channel_id=1, source_target_pairs={{0,1},{1,0},{2,3},{3,2},{4,5},{5,4},{6,7},{7,6},{8,9},{9,8},{10,11... | collective-permute-start | bytes 172040 | tf_op jit(solution)/shard_map/ppermute | solution.py:361
